TPU v7x, 128 devices: a whole 4x4x4 slice. The times are simulated.
128 devices in a mesh: member: 64 (over z, y, x), domain: 2 (over core).
Axes of the slice: x: 4, y: 4, z: 4, core: 2. Of those that a mesh axis runs over, the one named last changes fastest.
Arguments:
- state: bfloat16 [512, 131072], P('member', 'domain'), may hold values from -6 to 6
- predicted: bfloat16 [512, 262144], P('member', 'domain'), may hold values from -6 to 6
- perturbed: bfloat16 [512, 262144], P('member', 'domain'), may hold values from -6 to 6
- obs_weight: float32 [262144], P('domain'), may hold values from 0.3 to 3
- obs_position: int32 [262144], P('domain'), may hold values from 0 to 255
- row_count: int32 [2, 128], P(None, 'member'), may hold values from 256 to 2048
- row_index: int32 [2, 128, 2048], P('domain', 'member'), may hold values from 0 to 2047, as said below
Outputs:
- updated: bfloat16 [512, 131072], P('member', 'domain')
Inputs may be any that keep to these rules, and one draw needn't show every extreme that they name: `row_index`: for each block, 2048 distinct rows of its pool; only the first row_count of them are used.
All inputs are finite; a program needn't handle non-finite values.
Results may differ from a plain program's by a relative error of at most 0.0054.
Values may be sent and summed in bfloat16 or wider, within the bound.
No kernel may reach another device: no remote copies, remote signals or barrier semaphores. Data moves between devices by JAX's collectives and lax.ppermute only.
A program may use at most 128 MiB of HBM per device.

v0:
```python
import math

import jax
import jax.numpy as jnp
from jax import lax
from jax.sharding import PartitionSpec as P

SLAB = 256
NS_STEPS = 5
SPAN = 2


def scaled_rows(obs_pools, index_list, row_total, position, row_start, length):
    pred_pool, pert_pool, mean_pred, weight_pool, place_pool = obs_pools
    picked = lax.dynamic_slice_in_dim(index_list, row_start, length)
    pred_rows = jnp.take(pred_pool, picked, axis=0).astype(jnp.float32)
    pert_rows = jnp.take(pert_pool, picked, axis=0).astype(jnp.float32)
    offset = (jnp.take(place_pool, picked) - position).astype(jnp.float32) / SPAN
    taper_factor = 1.0 / (1.0 + offset * offset)
    live_rows = row_start + jnp.arange(length, dtype=jnp.int32) < row_total
    factor = jnp.where(live_rows, jnp.take(weight_pool, picked) * taper_factor, 0.0)
    members = pred_pool.shape[1]
    scaled = (
        factor[:, None]
        * (pred_rows - jnp.take(mean_pred, picked)[:, None])
        / jnp.sqrt(members - 1.0)
    ).astype(jnp.bfloat16)
    innovation = (factor[:, None] * (pert_rows - pred_rows)).astype(jnp.bfloat16)
    return (scaled, innovation)


def transpose_product(left_rows, right_rows):
    return lax.dot_general(
        left_rows, right_rows, (((0,), (0,)), ((), ())), preferred_element_type=jnp.float32
    )


def summed_products(slab_source, row_total, members):

    def add_slab(number, totals):
        scaled, innovation = slab_source(number * SLAB)
        return (
            totals[0] + transpose_product(scaled, scaled),
            totals[1] + transpose_product(scaled, innovation),
        )

    zero_sums = jnp.zeros((members, members), jnp.float32)
    return lax.fori_loop(0, (row_total + SLAB - 1) // SLAB, add_slab, (zero_sums, zero_sums))


def newton_inverse(gram_sum):
    members = gram_sum.shape[0]
    identity = jnp.eye(members, dtype=jnp.float32)
    system = identity + gram_sum
    spread = jnp.sqrt(jnp.sum(gram_sum * gram_sum))
    estimate = 2.0 / (2.0 + spread) * identity
    for iteration in range(NS_STEPS):
        product = jnp.dot(system, estimate, precision=lax.Precision.HIGHEST)
        estimate = jnp.dot(estimate, 2.0 * identity - product, precision=lax.Precision.HIGHEST)
    return estimate


def update_block(cell_block, gram_sum, cross_sum):
    members = gram_sum.shape[0]
    inverse = newton_inverse(gram_sum)
    weights = (
        jnp.dot(inverse, cross_sum, precision=lax.Precision.HIGHEST) / math.sqrt(members - 1.0)
    ).astype(jnp.bfloat16)
    values = cell_block.astype(jnp.float32)
    centred = (values - jnp.mean(values, axis=1, keepdims=True)).astype(jnp.bfloat16)
    return (values + jnp.dot(centred, weights, preferred_element_type=jnp.float32)).astype(
        jnp.bfloat16
    )


def per_device(state, predicted, perturbed, obs_weight, obs_position, row_count, row_index):
    cell_columns, pred_columns, pert_columns = (
        lax.all_to_all(state, "member", split_axis=1, concat_axis=0, tiled=True),
        lax.all_to_all(predicted, "member", split_axis=1, concat_axis=0, tiled=True),
        lax.all_to_all(perturbed, "member", split_axis=1, concat_axis=0, tiled=True),
    )
    cells_here = cell_columns.T
    pred_pool = pred_columns.T
    pert_pool = pert_columns.T
    groups = lax.axis_size("member")
    tile_total = lax.axis_size("domain")
    group_index = lax.axis_index("member")
    tile_index = lax.axis_index("domain")
    pool_rows = pred_pool.shape[0]
    members = pred_pool.shape[1]
    blocks = row_index.shape[1]
    block_cells = cells_here.shape[0] // blocks
    obs_pools = (
        pred_pool,
        pert_pool,
        jnp.mean(pred_pool, axis=1, dtype=jnp.float32),
        lax.dynamic_slice_in_dim(obs_weight, group_index * pool_rows, pool_rows),
        lax.dynamic_slice_in_dim(obs_position, group_index * pool_rows, pool_rows),
    )
    counts_here = lax.dynamic_index_in_dim(row_count, tile_index, 0, keepdims=False)
    first_block = (tile_index * groups + group_index) * blocks
    lists_here = row_index[0]
    partner = jnp.bitwise_xor(tile_index, tile_total // 2)
    partner_counts = lax.dynamic_index_in_dim(row_count, partner, 0, keepdims=False)
    own_load = jnp.sum(counts_here)
    partner_load = jnp.sum(partner_counts)
    sender = (own_load > partner_load) | (own_load == partner_load) & (tile_index < partner)
    moved_block = jnp.argmax(counts_here)
    lending = "none"
    returned = None
    renewed_blocks = []
    for block_number in range(blocks):
        give_away = sender & (moved_block == block_number)
        row_total = counts_here[block_number]
        local_total = row_total
        index_list = lists_here[block_number]
        position = first_block + block_number

        def slab_source(row_start, index_list=index_list, row_total=row_total, position=position):
            return scaled_rows(obs_pools, index_list, row_total, position, row_start, SLAB)

        gram_sum, cross_sum = summed_products(slab_source, local_total, members)
        cell_block = cells_here[block_number * block_cells : (block_number + 1) * block_cells]
        renewed_blocks.append(update_block(cell_block, gram_sum, cross_sum))
    renewed = jnp.concatenate(renewed_blocks, axis=0)
    return lax.all_to_all(renewed.T, "member", split_axis=0, concat_axis=1, tiled=True)


def solution(mesh):
    placed = (
        P("member", "domain"),
        P("member", "domain"),
        P("member", "domain"),
        P("domain"),
        P("domain"),
        P(None, "member"),
        P("domain", "member", None),
    )
    return jax.shard_map(
        per_device, mesh=mesh, in_specs=placed, out_specs=P("member", "domain"), check_vma=False
    )
```

profile of v0, /device:TPU:1, one launch (start us, length us, event | category | flops | bytes accessed | tf_op | source)
XLA Modules:
  0.0 398.1 jit_solution(9470250501183244003)
XLA Ops:
  0.0 29.8 %all_to_all.76 = bf16[8,64,1024]{2,0,1:T(8,128)(2,1)S(1)} all-to-all(bf16[8,64,1024]{2,0,1:T(8,128)(2,1)} %bitcast.69), channel_id=1, replica_groups=mesh['member'=64,'domain'=2] {'member'}, dimensions={1} | all-to-all | bytes 2097152 | tf_op jit(solution)/shard_map/all_to_all | solution.py:78
  29.8 32.1 %all_to_all.77 = bf16[8,64,2048]{2,0,1:T(8,128)(2,1)} all-to-all(bf16[8,64,2048]{2,0,1:T(8,128)(2,1)S(1)} %bitcast.67), channel_id=1, replica_groups=mesh['member'=64,'domain'=2] {'member'}, dimensions={1} | all-to-all | bytes 4194304 | tf_op jit(solution)/shard_map/all_to_all | solution.py:79
  61.9 6.8 %all-to-all-start.2 = ((bf16[8,64,2048]{2,0,1:T(8,128)(2,1)}), bf16[8,64,2048]{2,0,1:T(8,128)(2,1)}, u32[]{:S(2)}, u32[]{:S(2)}) async-start(bf16[8,64,2048]{2,0,1:T(8,128)(2,1)} %bitcast.68), calls=%async_computation.2 | async-start | bytes 4194304 | tf_op jit(solution)/shard_map/all_to_all | solution.py:80
  72.3 2.9 copy.13
  75.2 2.0 convert_reduce_fusion
  77.1 19.1 %all-to-all-done.2 = bf16[8,64,2048]{2,0,1:T(8,128)(2,1)} async-done(((bf16[8,64,2048]{2,0,1:T(8,128)(2,1)}), bf16[8,64,2048]{2,0,1:T(8,128)(2,1)}, u32[]{:S(2)}, u32[]{:S(2)}) %all-to-all-start.2) | async-done | bytes 2097184 | tf_op jit(solution)/shard_map/all_to_all | solution.py:80
  96.2 3.9 copy.14
  100.3 1.1 broadcast.66.clone.7
  101.4 43.5 %while.24 = (s32[]{:T(128)}, f32[512,512]{1,0:T(8,128)S(1)}, f32[512,512]{1,0:T(8,128)}, s32[]{:T(128)}, s32[]{:T(128)}, /*index=5*/s32[2048]{0:T(1024)S(1)}, f3...) while((s32[]{:T(128)}, f32[512,512]{1,0:T(8,128)S(1)}, ...), condition=%wide.region_3.7_spmd, body=%wide.region_2.0_spmd.sunk | while | flops 271456768 | bytes 6059223 | solution.py:48
  101.5 1.7 gather_fusion
  103.2 1.7 gather_fusion.1
  105.6 1.7 gather_fusion.2
  107.3 1.2 gather_fusion.3
  108.5 3.8 gather_fusion.4
  112.3 2.9 convolution_add_fusion.9
  115.8 1.7 gather_fusion
  117.6 1.7 gather_fusion.1
  120.0 1.7 gather_fusion.2
  121.7 1.2 gather_fusion.3
  122.9 3.8 gather_fusion.4
  126.6 2.9 convolution_add_fusion.9
  130.2 1.7 gather_fusion
  131.9 1.7 gather_fusion.1
  134.3 1.7 gather_fusion.2
  136.1 1.2 gather_fusion.3
  137.2 3.8 gather_fusion.4
  141.0 2.9 convolution_add_fusion.9
  146.5 1.8 select_subtract_fusion.11
  148.3 1.8 fusion.52
  150.2 1.9 select_subtract_fusion.10
  152.1 1.8 fusion.84
  153.9 1.9 select_subtract_fusion.9
  155.8 1.8 fusion.85
  157.7 1.9 select_subtract_fusion.8
  159.6 2.0 fusion.86
  161.6 1.9 select_subtract_fusion.7
  163.5 2.8 fusion.87
  166.4 1.1 broadcast.66.clone.5
  167.5 29.1 %while.25 = (s32[]{:T(128)}, f32[512,512]{1,0:T(8,128)S(1)}, f32[512,512]{1,0:T(8,128)}, s32[]{:T(128)}, s32[]{:T(128)}, /*index=5*/s32[2048]{0:T(1024)S(1)}, f3...) while((s32[]{:T(128)}, f32[512,512]{1,0:T(8,128)S(1)}, ...), condition=%wide.region_7.11_spmd, body=%wide.region_6.10_spmd.sunk | while | flops 271456768 | bytes 6059223 | solution.py:48
  167.6 1.7 gather_fusion.5
  169.4 1.7 gather_fusion.6
  171.9 1.7 gather_fusion.7
  173.6 1.2 gather_fusion.8
  174.8 3.8 gather_fusion.9
  178.5 2.8 convolution_add_fusion.11
  182.1 1.7 gather_fusion.5
  183.8 1.7 gather_fusion.6
  186.3 1.7 gather_fusion.7
  188.1 1.2 gather_fusion.8
  189.2 3.8 gather_fusion.9
  193.0 2.8 convolution_add_fusion.11
  198.2 1.8 select_subtract_fusion.6
  200.0 1.8 fusion.46
  201.8 1.9 select_subtract_fusion.5
  203.7 1.9 fusion.88
  205.6 1.9 select_subtract_fusion.4
  207.5 1.9 fusion.89
  209.3 1.9 select_subtract_fusion.3
  211.3 2.1 fusion.90
  213.4 1.9 select_subtract_fusion.2
  215.3 1.9 fusion.91
  217.2 1.9 fusion.58
  219.6 1.9 fusion.59
  222.5 174.1 %all_to_all.78 = bf16[64,8,1024]{2,1,0:T(8,128)(2,1)S(1)} all-to-all(bf16[64,8,1024]{2,1,0:T(8,128)(2,1)S(1)} %bitcast.65), channel_id=1, replica_groups=mesh['member'=64,'domain'=2] {'member'}, dimensions={0} | all-to-all | bytes 2097152 | tf_op jit(solution)/shard_map/all_to_all | solution.py:126
  (61 shorter events, 13.6 us)
Async XLA Ops:
  0.0 68.7 %copy-start = (s32[2,2]{1,0:T(2,128)S(1)}, s32[2,2]{1,0:T(2,128)}, u32[]{:S(2)}) copy-start(s32[2,2]{1,0:T(2,128)} %param.22) | copy-start | bytes 52
  0.0 29.8 %copy-start.6 = (bf16[8,131072]{1,0:T(8,128)(2,1)S(1)}, bf16[8,131072]{1,0:T(8,128)(2,1)}, u32[]{:S(2)}) copy-start(bf16[8,131072]{1,0:T(8,128)(2,1)} %param.18) | copy-start | bytes 6291460
  61.9 8.8 %copy-start.7 = (s32[1,2,2048]{2,1,0:T(2,128)S(1)}, s32[1,2,2048]{2,1,0:T(2,128)}, u32[]{:S(2)}) copy-start(s32[1,2,2048]{2,1,0:T(2,128)} %param.23) | copy-start | bytes 49156
  61.9 34.3 %all-to-all-start.2 = ((bf16[8,64,2048]{2,0,1:T(8,128)(2,1)}), bf16[8,64,2048]{2,0,1:T(8,128)(2,1)}, u32[]{:S(2)}, u32[]{:S(2)}) async-start(bf16[8,64,2048]{2,0,1:T(8,128)(2,1)} %bitcast.68), calls=%async_computation.2 | async-start | bytes 4194304 | tf_op jit(solution)/shard_map/all_to_all | solution.py:80
  71.3 1.0 copy-start.4
  100.1 1.2 dynamic-slice-start
  100.1 1.2 dynamic-slice-start.1
  215.3 1.9 copy-start.2
  215.3 1.9 copy-start.3
  217.2 1.9 copy-start.5
  217.2 2.4 copy-start.1
where the time goes:
time: 401 us; the launch traced here: 398 us
  blocking collectives  236 us (59%)
  local copies, waits for them, and re-layouts  63.2 us (16%)
  matrix products  60.5 us (15%)
  waiting for transfers between devices  19.1 us (5%)
  other arithmetic  7.98 us (2%)
  starting transfers between devices  6.79 us (2%)
    all_to_all x1, blocking collectives, per_device(): lax.all_to_all(renewed.T, 'member', split_axis=0, concat_axis=1, tiled=True)  174 us
    all_to_all x1, blocking collectives, per_device(): lax.all_to_all(predicted, 'member', split_axis=1, concat_axis=0, tiled=True)  32.1 us
    all_to_all x1, blocking collectives, per_device(): lax.all_to_all(state, 'member', split_axis=1, concat_axis=0, tiled=True)  29.8 us
    dot_general x10, matrix products, newton_inverse(): jnp.dot(estimate, 2.0 * identity - product, precision=lax.Precision.HIGHEST)  19.9 us
    all_to_all x1, waiting for transfers between devices, per_device(): lax.all_to_all(perturbed, 'member', split_axis=1, concat_axis=0, tiled=True)  19.1 us
    gather x5, local copies, waits for them, and re-layouts, scaled_rows(): pert_rows = jnp.take(pert_pool, picked, axis=0).astype(jnp.float32)  18.9 us
    dot_general x10, matrix products, newton_inverse(): product = jnp.dot(system, estimate, precision=lax.Precision.HIGHEST)  18.7 us
    dot_general x10, matrix products, transpose_product(): lax.dot_general(left_rows, right_rows, (((0,), (0,)), ((), ())), preferre...  17.2 us
  transfers between devices with their start and end apart: 1, of which 1 were waited for; matrix products, arithmetic and copies ran while one was open for 2% of the time, Pallas kernels for 0%

commit v1 on v0

v1 whole, which is shorter than its diff:
```python
import math

import jax
import jax.numpy as jnp
from jax import lax
from jax.experimental import pallas as pl
from jax.experimental.pallas import tpu as pltpu
from jax.sharding import PartitionSpec as P

NS_STEPS = 5
SPAN = 2
LANES = 128

f32 = jnp.float32
bf16 = jnp.bfloat16


def contract_lanes(left, right):
    return lax.dot_general(left, right, (((1,), (1,)), ((), ())), preferred_element_type=f32)


def dot(left, right):
    return jnp.dot(left, right, preferred_element_type=f32)


def split(value):
    high = value.astype(bf16)
    return high, (value - high.astype(f32)).astype(bf16)


def dot3(left, right):
    left_high, left_low = left
    right_high, right_low = right
    return dot(left_high, right_high) + (dot(left_high, right_low) + dot(left_low, right_high))


def factor_kernel(scalars, index, weight, place, factor_out):
    blocks, rows = index.shape
    tiles = rows // LANES
    for block in range(blocks):
        listed = index[block : block + 1, :]
        live = lax.broadcasted_iota(jnp.int32, (1, rows), 1) < scalars[1 + block]
        high = jnp.where(live, listed // LANES, -1)
        low = listed % LANES
        high_hot = (lax.broadcasted_iota(jnp.int32, (tiles, rows), 0) == high).astype(f32).astype(bf16)
        low_hot = (lax.broadcasted_iota(jnp.int32, (LANES, rows), 0) == low).astype(f32).astype(bf16)
        chosen = contract_lanes(high_hot, low_hot)
        chosen = jnp.concatenate([chosen[t : t + 1, :] for t in range(tiles)], axis=1)
        offset = (place[...] - (scalars[0] + block)).astype(f32) / SPAN
        taper = 1.0 / (1.0 + offset * offset)
        factor_out[block : block + 1, :] = jnp.where(chosen > 0.5, weight[...] * taper, 0.0)


def inverse_kernel(pred, factor, scaled_out, inverse_out):
    members = pred.shape[0]
    blocks = factor.shape[0]
    values = pred[...].astype(f32)
    deviation = values - jnp.mean(values, axis=0, keepdims=True)
    eye = (
        lax.broadcasted_iota(jnp.int32, (members, members), 0)
        == lax.broadcasted_iota(jnp.int32, (members, members), 1)
    ).astype(f32)
    for block in range(blocks):
        scaled = (factor[block : block + 1, :] * deviation * (1.0 / math.sqrt(members - 1.0))).astype(bf16)
        scaled_out[block] = scaled
        gram = contract_lanes(scaled, scaled)
        start = 2.0 / (2.0 + jnp.sqrt(jnp.sum(gram * gram)))
        residual = eye - start * (eye + gram)
        estimate = eye + residual
        residual_parts = split(residual)
        for step in range(1, NS_STEPS):
            residual = dot3(residual_parts, residual_parts)
            residual_parts = split(residual)
            estimate = estimate + dot3(split(estimate), residual_parts)
        inverse_out[block] = start * estimate


def weights_kernel(pred, pert, factor, scaled, inverse, weights_out):
    members = pred.shape[0]
    change = pert[...].astype(f32) - pred[...].astype(f32)
    for block in range(factor.shape[0]):
        innovation = (factor[block : block + 1, :] * change).astype(bf16)
        cross_t = contract_lanes(innovation, scaled[block])
        weights_t = dot3(split(cross_t), split(inverse[block]))
        weights_out[block] = (weights_t * (1.0 / math.sqrt(members - 1.0))).astype(bf16)


def update_kernel(cells, weights_t, updated):
    blocks = weights_t.shape[0]
    width = cells.shape[1] // blocks
    for block in range(blocks):
        span = slice(block * width, (block + 1) * width)
        values = cells[:, span].astype(f32)
        centred = (values - jnp.mean(values, axis=0, keepdims=True)).astype(bf16)
        updated[:, span] = (values + dot(weights_t[block], centred)).astype(bf16)


def call(kernel, outs, flops, scalars=0):
    vmem = pl.BlockSpec(memory_space=pltpu.VMEM)
    smem = pl.BlockSpec(memory_space=pltpu.SMEM)

    def run(*args):
        return pl.pallas_call(
            kernel,
            out_shape=outs,
            in_specs=[smem] * scalars + [vmem] * (len(args) - scalars),
            out_specs=jax.tree.map(lambda _: vmem, outs),
            cost_estimate=pl.CostEstimate(flops=flops, transcendentals=0, bytes_accessed=1 << 22),
            name=kernel.__name__,
        )(*args)

    return run


def per_device(state, predicted, perturbed, obs_weight, obs_position, row_count, row_index):
    exchange = lambda value: lax.all_to_all(value, "member", split_axis=1, concat_axis=0, tiled=True)
    groups = lax.axis_size("member")
    group_index = lax.axis_index("member")
    tile_index = lax.axis_index("domain")
    blocks = row_index.shape[1]
    members = state.shape[0] * groups
    rows = predicted.shape[1] // groups

    pred_pool = exchange(predicted)
    pert_pool = exchange(perturbed)
    cells = exchange(state)

    counts = lax.dynamic_index_in_dim(row_count, tile_index, 0, keepdims=False)
    first_block = (tile_index * groups + group_index) * blocks
    scalars = jnp.concatenate([first_block[None].astype(jnp.int32), counts])
    weight = lax.dynamic_slice_in_dim(obs_weight, group_index * rows, rows)[None]
    place = lax.dynamic_slice_in_dim(obs_position, group_index * rows, rows)[None]

    shaped = jax.ShapeDtypeStruct
    cube = 2 * blocks * members**3
    factor = call(factor_kernel, shaped((blocks, rows), f32), cube // 4, 1)(scalars, row_index[0], weight, place)
    scaled, inverse = call(
        inverse_kernel,
        (shaped((blocks, members, rows), bf16), shaped((blocks, members, members), f32)),
        30 * cube,
    )(pred_pool, factor)
    weights_t = call(weights_kernel, shaped((blocks, members, members), bf16), 7 * cube)(
        pred_pool, pert_pool, factor, scaled, inverse
    )
    updated = call(update_kernel, shaped(cells.shape, bf16), cube)(cells, weights_t)
    return lax.all_to_all(updated, "member", split_axis=0, concat_axis=1, tiled=True)


def solution(mesh):
    placed = (
        P("member", "domain"),
        P("member", "domain"),
        P("member", "domain"),
        P("domain"),
        P("domain"),
        P(None, "member"),
        P("domain", "member", None),
    )
    return jax.shard_map(
        per_device, mesh=mesh, in_specs=placed, out_specs=P("member", "domain"), check_vma=False
    )
```

time: 401 us -> 148 us (0.37)
  the two profiles are of different devices: /device:TPU:1 before, /device:TPU:0 now
where the time goes in v1:
time: 148 us; the launch traced here: 147 us
  blocking collectives  70.2 us (47%)
  Pallas kernels  35.2 us (24%)
  waiting for transfers between devices  24.8 us (17%)
  starting transfers between devices  11.9 us (8%)
  local copies, waits for them, and re-layouts  4.54 us (3%)
    all_to_all x1, blocking collectives, per_device(): lax.all_to_all(value, 'member', split_axis=1, concat_axis=0, tiled=True)  41.7 us
    pallas_call x4, Pallas kernels, run(): pl.pallas_call(kernel, out_shape=outs, in_specs=[smem] * scalars + [vmem]...  35.2 us
    all_to_all x1, blocking collectives, per_device(): lax.all_to_all(updated, 'member', split_axis=0, concat_axis=1, tiled=True)  28.5 us
    all_to_all x2, waiting for transfers between devices, per_device(): lax.all_to_all(value, 'member', split_axis=1, concat_axis=0, tiled=True)  24.8 us
    all_to_all x2, starting transfers between devices, per_device(): lax.all_to_all(value, 'member', split_axis=1, concat_axis=0, tiled=True)  11.9 us
  transfers between devices with their start and end apart: 2, of which 1 were waited for; matrix products, arithmetic and copies ran while one was open for 2% of the time, Pallas kernels for 22%

profile of v1, /device:TPU:0, one launch (start us, length us, event | category | flops | bytes accessed | tf_op | source)
XLA Modules:
  0.0 147.3 jit_solution(15229545886515463131)
XLA Ops:
  0.0 0.0 copy-start
  0.0 41.7 %all_to_all.76 = bf16[8,64,2048]{2,0,1:T(8,128)(2,1)} all-to-all(bf16[8,64,2048]{2,0,1:T(8,128)(2,1)} %bitcast.25), channel_id=1, replica_groups=mesh['member'=64,'domain'=2] {'member'}, dimensions={1} | all-to-all | bytes 4194304 | tf_op jit(solution)/shard_map/all_to_all | solution.py:116
  41.7 5.8 %all-to-all-start.2 = ((bf16[8,64,2048]{2,0,1:T(8,128)(2,1)}), bf16[8,64,2048]{2,0,1:T(8,128)(2,1)S(1)}, u32[]{:S(2)}, u32[]{:S(2)}) async-start(bf16[8,64,2048]{2,0,1:T(8,128)(2,1)} %bitcast.6), calls=%async_computation.2 | async-start | bytes 4194304 | tf_op jit(solution)/shard_map/all_to_all | solution.py:116
  47.6 1.3 dynamic_slice.11
  48.9 1.3 dynamic_slice.12
  50.2 0.0 copy-done
  50.2 0.6 pad_add_fusion.scalars
  50.8 1.8 %factor_kernel.1.factor = f32[2,2048]{1,0:T(2,128)} custom-call(s32[3]{0:T(128)} %pad_add_fusion.scalars, s32[2,2048]{1,0:T(2,128)} %bitcast.32, f32[1,2048]{1,0:T(1,128)} %bitcast.30, s32[1,2048]{1,0:T(1,128)} %bitcast.31), custom_call_target="tpu_custom_call" | custom-call | flops 134217728 | bytes 4194304 | tf_op jit(solution)/shard_map/factor_kernel/pallas_call | solution.py:103
  52.6 24.8 %all-to-all-done.2 = bf16[8,64,2048]{2,0,1:T(8,128)(2,1)S(1)} async-done(((bf16[8,64,2048]{2,0,1:T(8,128)(2,1)}), bf16[8,64,2048]{2,0,1:T(8,128)(2,1)S(1)}, u32[]{:S(2)}, u32[]{:S(2)}) %all-to-all-start.2) | async-done | bytes 2097184 | tf_op jit(solution)/shard_map/all_to_all | solution.py:116
  77.4 0.0 copy-start.2
  77.4 6.0 %all-to-all-start = ((bf16[8,64,1024]{2,0,1:T(8,128)(2,1)}), bf16[8,64,1024]{2,0,1:T(8,128)(2,1)S(1)}, u32[]{:S(2)}, u32[]{:S(2)}) async-start(bf16[8,64,1024]{2,0,1:T(8,128)(2,1)} %bitcast.29), calls=%async_computation | async-start | bytes 2097152 | tf_op jit(solution)/shard_map/all_to_all | solution.py:116
  83.4 21.0 %inverse_kernel.1 = (bf16[2,512,2048]{2,1,0:T(8,128)(2,1)}, f32[2,512,512]{2,1,0:T(8,128)}) custom-call(bf16[512,2048]{1,0:T(8,128)(2,1)} %bitcast.26, f32[2,2048]{1,0:T(2,128)} %factor_kernel.1.factor), custom_call_target="tpu_custom_call" | custom-call | flops 16106127360 | bytes 4194304 | tf_op jit(solution)/shard_map/inverse_kernel/pallas_call | solution.py:103
  104.4 0.0 copy-done.2
  104.4 9.0 %weights_kernel.1.weights_t = bf16[2,512,512]{2,1,0:T(8,128)(2,1)} custom-call(bf16[512,2048]{1,0:T(8,128)(2,1)} %bitcast.27, bf16[512,2048]{1,0:T(8,128)(2,1)} %bitcast.28, f32[2,2048]{1,0:T(2,128)} %factor_kernel.1.factor, bf16[2,512,2048]{2,1,0:T(8,128)(2,1)} %get-tuple-element.7.scaled, f32[2,512,512]{2,1,0:T(8,128)} %get-tuple-element.8.inverse), custom_call_target="tpu_custom_call" | custom-call | flops 3758096384 | bytes 4194304 | tf_op jit(solution)/shard_map/weights_kernel/pallas_call | solution.py:103
  113.5 0.0 all-to-all-done
  113.5 0.0 copy-start.1
  113.5 1.0 copy-done.1
  114.5 3.3 %update_kernel.1 = bf16[512,1024]{1,0:T(8,128)(2,1)} custom-call(bf16[512,1024]{1,0:T(8,128)(2,1)} %bitcast.22, bf16[2,512,512]{2,1,0:T(8,128)(2,1)} %weights_kernel.1.weights_t), custom_call_target="tpu_custom_call" | custom-call | flops 536870912 | bytes 4194304 | tf_op jit(solution)/shard_map/update_kernel/pallas_call | solution.py:103
  117.8 28.5 %all_to_all.77 = bf16[64,8,1024]{2,1,0:T(8,128)(2,1)S(1)} all-to-all(bf16[64,8,1024]{2,1,0:T(8,128)(2,1)} %bitcast.23), channel_id=1, replica_groups=mesh['member'=64,'domain'=2] {'member'}, dimensions={0} | all-to-all | bytes 2097152 | tf_op jit(solution)/shard_map/all_to_all | solution.py:146
  146.3 1.0 copy.9
  (1 shorter events, 0.0 us)
Async XLA Ops:
  0.0 50.2 %copy-start = (s32[2,2]{1,0:T(2,128)S(1)}, s32[2,2]{1,0:T(2,128)}, u32[]{:S(2)}) copy-start(s32[2,2]{1,0:T(2,128)} %param.12) | copy-start | bytes 52
  41.7 35.7 %all-to-all-start.2 = ((bf16[8,64,2048]{2,0,1:T(8,128)(2,1)}), bf16[8,64,2048]{2,0,1:T(8,128)(2,1)S(1)}, u32[]{:S(2)}, u32[]{:S(2)}) async-start(bf16[8,64,2048]{2,0,1:T(8,128)(2,1)} %bitcast.6), calls=%async_computation.2 | async-start | bytes 4194304 | tf_op jit(solution)/shard_map/all_to_all | solution.py:116
  77.4 27.0 %copy-start.2 = (bf16[8,64,2048]{2,0,1:T(8,128)(2,1)}, bf16[8,64,2048]{2,0,1:T(8,128)(2,1)S(1)}, u32[]{:S(2)}) copy-start(bf16[8,64,2048]{2,0,1:T(8,128)(2,1)S(1)} %all-to-all-done.2) | copy-start | bytes 6291460
  77.4 36.1 %all-to-all-start = ((bf16[8,64,1024]{2,0,1:T(8,128)(2,1)}), bf16[8,64,1024]{2,0,1:T(8,128)(2,1)S(1)}, u32[]{:S(2)}, u32[]{:S(2)}) async-start(bf16[8,64,1024]{2,0,1:T(8,128)(2,1)} %bitcast.29), calls=%async_computation | async-start | bytes 2097152 | tf_op jit(solution)/shard_map/all_to_all | solution.py:116
  113.5 1.0 copy-start.1

commit v2 on v1

--- a/solution.py
+++ b/solution.py
@@ -17,6 +17,10 @@
 
 def contract_lanes(left, right):
     return lax.dot_general(left, right, (((1,), (1,)), ((), ())), preferred_element_type=f32)
+
+
+def contract_rows(left, right):
+    return lax.dot_general(left, right, (((0,), (0,)), ((), ())), preferred_element_type=f32)
 
 
 def dot(left, right):
@@ -51,10 +55,11 @@
         factor_out[block : block + 1, :] = jnp.where(chosen > 0.5, weight[...] * taper, 0.0)
 
 
-def inverse_kernel(pred, factor, scaled_out, inverse_out):
-    members = pred.shape[0]
-    blocks = factor.shape[0]
-    values = pred[...].astype(f32)
+def gain_kernel(first, factor, gain_out):
+    members = first.shape[0]
+    blocks, rows = factor.shape
+    width = (first.shape[1] - rows) // blocks
+    values = first[:, :rows].astype(f32)
     deviation = values - jnp.mean(values, axis=0, keepdims=True)
     eye = (
         lax.broadcasted_iota(jnp.int32, (members, members), 0)
@@ -62,7 +67,6 @@
     ).astype(f32)
     for block in range(blocks):
         scaled = (factor[block : block + 1, :] * deviation * (1.0 / math.sqrt(members - 1.0))).astype(bf16)
-        scaled_out[block] = scaled
         gram = contract_lanes(scaled, scaled)
         start = 2.0 / (2.0 + jnp.sqrt(jnp.sum(gram * gram)))
         residual = eye - start * (eye + gram)
@@ -72,27 +76,23 @@
             residual = dot3(residual_parts, residual_parts)
             residual_parts = split(residual)
             estimate = estimate + dot3(split(estimate), residual_parts)
-        inverse_out[block] = start * estimate
+        cells = first[:, rows + block * width : rows + (block + 1) * width].astype(f32)
+        centred = (cells - jnp.mean(cells, axis=0, keepdims=True)).astype(bf16)
+        high, low = split(estimate * (start * (1.0 / math.sqrt(members - 1.0))))
+        smoothed_high, smoothed_low = split(dot(high, centred) + dot(low, centred))
+        gain_out[block] = (
+            contract_rows(scaled, smoothed_high) + contract_rows(scaled, smoothed_low)
+        ).astype(bf16)
 
 
-def weights_kernel(pred, pert, factor, scaled, inverse, weights_out):
-    members = pred.shape[0]
-    change = pert[...].astype(f32) - pred[...].astype(f32)
-    for block in range(factor.shape[0]):
+def update_kernel(first, pert, factor, gain, updated):
+    blocks, rows = factor.shape
+    width = (first.shape[1] - rows) // blocks
+    change = pert[...].astype(f32) - first[:, :rows].astype(f32)
+    for block in range(blocks):
         innovation = (factor[block : block + 1, :] * change).astype(bf16)
-        cross_t = contract_lanes(innovation, scaled[block])
-        weights_t = dot3(split(cross_t), split(inverse[block]))
-        weights_out[block] = (weights_t * (1.0 / math.sqrt(members - 1.0))).astype(bf16)
-
-
-def update_kernel(cells, weights_t, updated):
-    blocks = weights_t.shape[0]
-    width = cells.shape[1] // blocks
-    for block in range(blocks):
-        span = slice(block * width, (block + 1) * width)
-        values = cells[:, span].astype(f32)
-        centred = (values - jnp.mean(values, axis=0, keepdims=True)).astype(bf16)
-        updated[:, span] = (values + dot(weights_t[block], centred)).astype(bf16)
+        cells = first[:, rows + block * width : rows + (block + 1) * width].astype(f32)
+        updated[:, block * width : (block + 1) * width] = (cells + dot(innovation, gain[block])).astype(bf16)
 
 
 def call(kernel, outs, flops, scalars=0):
@@ -113,17 +113,22 @@
 
 
 def per_device(state, predicted, perturbed, obs_weight, obs_position, row_count, row_index):
-    exchange = lambda value: lax.all_to_all(value, "member", split_axis=1, concat_axis=0, tiled=True)
+    exchange = lambda value: lax.all_to_all(
+        value.reshape(value.shape[0], groups, -1), "member", split_axis=1, concat_axis=0, tiled=True
+    ).reshape(members, -1)
     groups = lax.axis_size("member")
     group_index = lax.axis_index("member")
     tile_index = lax.axis_index("domain")
     blocks = row_index.shape[1]
-    members = state.shape[0] * groups
+    held = state.shape[0]
+    members = held * groups
     rows = predicted.shape[1] // groups
+    cells = state.shape[1] // groups
 
-    pred_pool = exchange(predicted)
-    pert_pool = exchange(perturbed)
-    cells = exchange(state)
+    paired = jnp.concatenate(
+        [predicted.reshape(held, groups, rows), state.reshape(held, groups, cells)], axis=2
+    )
+    first = exchange(paired)
 
     counts = lax.dynamic_index_in_dim(row_count, tile_index, 0, keepdims=False)
     first_block = (tile_index * groups + group_index) * blocks
@@ -133,16 +138,11 @@
 
     shaped = jax.ShapeDtypeStruct
     cube = 2 * blocks * members**3
-    factor = call(factor_kernel, shaped((blocks, rows), f32), cube // 4, 1)(scalars, row_index[0], weight, place)
-    scaled, inverse = call(
-        inverse_kernel,
-        (shaped((blocks, members, rows), bf16), shaped((blocks, members, members), f32)),
-        30 * cube,
-    )(pred_pool, factor)
-    weights_t = call(weights_kernel, shaped((blocks, members, members), bf16), 7 * cube)(
-        pred_pool, pert_pool, factor, scaled, inverse
-    )
-    updated = call(update_kernel, shaped(cells.shape, bf16), cube)(cells, weights_t)
+    factor = call(factor_kernel, shaped((blocks, rows), f32), cube, 1)(scalars, row_index[0], weight, place)
+    factor, perturbed = lax.optimization_barrier((factor, perturbed))
+    pert_pool = exchange(perturbed)
+    gain = call(gain_kernel, shaped((blocks, rows, cells // blocks), bf16), 40 * cube)(first, factor)
+    updated = call(update_kernel, shaped((members, cells), bf16), 4 * cube)(first, pert_pool, factor, gain)
     return lax.all_to_all(updated, "member", split_axis=0, concat_axis=1, tiled=True)
 
 

time: 148 us -> 129 us (0.87)
  blocking collectives: 70.2 us -> 26.5 us
  waiting for transfers between devices: 24.8 us -> 38.8 us
  starting transfers between devices: 11.9 us -> 18.9 us
  other arithmetic: 0.64 us -> 4.43 us
    all_to_all x1 -> x0, blocking collectives: 41.7 us -> none  [per_device(): lax.all_to_all(value, 'member', split_axis=1, concat_axis=0, tiled=True)]
    all_to_all x2, waiting for transfers between devices: 24.8 us -> 38.8 us  [per_device(): lax.all_to_all(value.reshape(value.shape[0], groups, -1), 'member', split...]
    all_to_all x2, starting transfers between devices: 11.9 us -> 18.9 us  [per_device(): lax.all_to_all(value.reshape(value.shape[0], groups, -1), 'member', split...]
    concatenate x0 -> x1, other arithmetic: none -> 3.84 us  [per_device(): jnp.concatenate([predicted.reshape(held, groups, rows), state.reshape(hel...]
    all_to_all x1, blocking collectives: 28.5 us -> 26.5 us  [per_device(): lax.all_to_all(updated, 'member', split_axis=0, concat_axis=1, tiled=True)]
    pallas_call x4 -> x3, Pallas kernels: 35.2 us -> 36.5 us  [run(): pl.pallas_call(kernel, out_shape=outs, in_specs=[smem] * scalars + [vmem]...]
  transfers between devices with their start and end apart: 2 -> 2, of which waited for: 1 -> 2; matrix products, arithmetic and copies ran while one was open for 2% -> 2% of each run, Pallas kernels for 22% -> 23%
where the time goes in v2:
time: 129 us
  waiting for transfers between devices  38.8 us (30%)
  Pallas kernels  36.5 us (28%)
  blocking collectives  26.5 us (21%)
  starting transfers between devices  18.9 us (15%)
  other arithmetic  4.43 us (3%)
  local copies, waits for them, and re-layouts  3.57 us (3%)
    all_to_all x2, waiting for transfers between devices, per_device(): lax.all_to_all(value.reshape(value.shape[0], groups, -1), 'member', split...  38.8 us
    pallas_call x3, Pallas kernels, run(): pl.pallas_call(kernel, out_shape=outs, in_specs=[smem] * scalars + [vmem]...  36.5 us
    all_to_all x1, blocking collectives, per_device(): lax.all_to_all(updated, 'member', split_axis=0, concat_axis=1, tiled=True)  26.5 us
    all_to_all x2, starting transfers between devices, per_device(): lax.all_to_all(value.reshape(value.shape[0], groups, -1), 'member', split...  18.9 us
    concatenate x1, other arithmetic, per_device(): jnp.concatenate([predicted.reshape(held, groups, rows), state.reshape(hel...  3.84 us
  transfers between devices with their start and end apart: 2, of which 2 were waited for; matrix products, arithmetic and copies ran while one was open for 2% of the time, Pallas kernels for 23%

profile of v2, /device:TPU:0, one launch (start us, length us, event | category | flops | bytes accessed | tf_op | source)
XLA Modules:
  0.0 128.7 jit_solution(6111322719411045742)
XLA Ops:
  0.0 0.0 copy-start
  0.0 3.8 %pad_maximum_fusion = bf16[8,64,3072]{2,0,1:T(8,128)(2,1)} fusion(bf16[8,64,1024]{2,0,1:T(8,128)(2,1)} %bitcast.29, bf16[8,64,2048]{2,0,1:T(8,128)(2,1)} %bitcast.27), kind=kLoop, calls=%fused_computation | loop fusion | flops 6291456 | bytes 6291456 | tf_op jit(solution)/shard_map/concatenate | solution.py:128
  3.8 11.5 %all-to-all-start = ((bf16[8,64,3072]{2,0,1:T(8,128)(2,1)}), bf16[8,64,3072]{2,0,1:T(8,128)(2,1)S(1)}, u32[]{:S(2)}, u32[]{:S(2)}) async-start(bf16[8,64,3072]{2,0,1:T(8,128)(2,1)} %pad_maximum_fusion), calls=%async_computation | async-start | bytes 6291456 | tf_op jit(solution)/shard_map/all_to_all | solution.py:116
  15.4 1.3 %dynamic_slice.11 = f32[2048]{0:T(1024)} dynamic-slice(f32[131072]{0:T(1024)} %param.10, s32[]{:T(128)S(6)} %select_n.9), dynamic_slice_sizes={2048} | dynamic-slice | bytes 16388 | tf_op jit(solution)/shard_map/dynamic_slice | solution.py:136
  16.7 1.3 dynamic_slice.12
  18.0 0.0 copy-done
  18.0 0.6 pad_add_fusion.scalars
  18.6 1.8 %factor_kernel.1.factor = f32[2,2048]{1,0:T(2,128)} custom-call(s32[3]{0:T(128)} %pad_add_fusion.scalars, s32[2,2048]{1,0:T(2,128)} %bitcast.32, f32[1,2048]{1,0:T(1,128)} %bitcast.30, s32[1,2048]{1,0:T(1,128)} %bitcast.31), custom_call_target="tpu_custom_call" | custom-call | flops 536870912 | bytes 4194304 | tf_op jit(solution)/shard_map/factor_kernel/pallas_call | solution.py:103
  20.4 36.5 %all-to-all-done = bf16[8,64,3072]{2,0,1:T(8,128)(2,1)S(1)} async-done(((bf16[8,64,3072]{2,0,1:T(8,128)(2,1)}), bf16[8,64,3072]{2,0,1:T(8,128)(2,1)S(1)}, u32[]{:S(2)}, u32[]{:S(2)}) %all-to-all-start) | async-done | bytes 3145760 | tf_op jit(solution)/shard_map/all_to_all | solution.py:116
  56.9 0.0 copy-start.1
  56.9 7.4 %all-to-all-start.1 = ((bf16[8,64,2048]{2,0,1:T(8,128)(2,1)}), bf16[8,64,2048]{2,0,1:T(8,128)(2,1)}, u32[]{:S(2)}, u32[]{:S(2)}) async-start(bf16[8,64,2048]{2,0,1:T(8,128)(2,1)} %bitcast.28), calls=%async_computation.1 | async-start | bytes 4194304 | tf_op jit(solution)/shard_map/all_to_all | solution.py:116
  64.3 0.0 copy-done.1
  64.3 27.6 %gain_kernel.1.gain = bf16[2,2048,512]{2,1,0:T(8,128)(2,1)} custom-call(bf16[512,3072]{1,0:T(8,128)(2,1)} %bitcast.23, f32[2,2048]{1,0:T(2,128)} %factor_kernel.1.factor), custom_call_target="tpu_custom_call" | custom-call | flops 21474836480 | bytes 4194304 | tf_op jit(solution)/shard_map/gain_kernel/pallas_call | solution.py:103
  91.9 2.3 %all-to-all-done.1 = bf16[8,64,2048]{2,0,1:T(8,128)(2,1)} async-done(((bf16[8,64,2048]{2,0,1:T(8,128)(2,1)}), bf16[8,64,2048]{2,0,1:T(8,128)(2,1)}, u32[]{:S(2)}, u32[]{:S(2)}) %all-to-all-start.1) | async-done | bytes 2097184 | tf_op jit(solution)/shard_map/all_to_all | solution.py:116
  94.2 7.1 %update_kernel.1 = bf16[512,1024]{1,0:T(8,128)(2,1)} custom-call(bf16[512,3072]{1,0:T(8,128)(2,1)} %bitcast.24, bf16[512,2048]{1,0:T(8,128)(2,1)} %bitcast.13.pert, f32[2,2048]{1,0:T(2,128)} %factor_kernel.1.factor, bf16[2,2048,512]{2,1,0:T(8,128)(2,1)} %gain_kernel.1.gain), custom_call_target="tpu_custom_call" | custom-call | flops 2147483648 | bytes 4194304 | tf_op jit(solution)/shard_map/update_kernel/pallas_call | solution.py:103
  101.3 26.5 %all_to_all.49 = bf16[64,8,1024]{2,1,0:T(8,128)(2,1)S(1)} all-to-all(bf16[64,8,1024]{2,1,0:T(8,128)(2,1)} %bitcast.25), channel_id=1, replica_groups=mesh['member'=64,'domain'=2] {'member'}, dimensions={0} | all-to-all | bytes 2097152 | tf_op jit(solution)/shard_map/all_to_all | solution.py:146
  127.8 1.0 copy.9
  (1 shorter events, 0.0 us)
Async XLA Ops:
  0.0 18.0 %copy-start = (s32[2,2]{1,0:T(2,128)S(1)}, s32[2,2]{1,0:T(2,128)}, u32[]{:S(2)}) copy-start(s32[2,2]{1,0:T(2,128)} %param.12) | copy-start | bytes 52
  3.8 53.1 %all-to-all-start = ((bf16[8,64,3072]{2,0,1:T(8,128)(2,1)}), bf16[8,64,3072]{2,0,1:T(8,128)(2,1)S(1)}, u32[]{:S(2)}, u32[]{:S(2)}) async-start(bf16[8,64,3072]{2,0,1:T(8,128)(2,1)} %pad_maximum_fusion), calls=%async_computation | async-start | bytes 6291456 | tf_op jit(solution)/shard_map/all_to_all | solution.py:116
  56.9 7.4 %copy-start.1 = (bf16[8,64,3072]{2,0,1:T(8,128)(2,1)}, bf16[8,64,3072]{2,0,1:T(8,128)(2,1)S(1)}, u32[]{:S(2)}) copy-start(bf16[8,64,3072]{2,0,1:T(8,128)(2,1)S(1)} %all-to-all-done) | copy-start | bytes 9437188
  56.9 37.3 %all-to-all-start.1 = ((bf16[8,64,2048]{2,0,1:T(8,128)(2,1)}), bf16[8,64,2048]{2,0,1:T(8,128)(2,1)}, u32[]{:S(2)}, u32[]{:S(2)}) async-start(bf16[8,64,2048]{2,0,1:T(8,128)(2,1)} %bitcast.28), calls=%async_computation.1 | async-start | bytes 4194304 | tf_op jit(solution)/shard_map/all_to_all | solution.py:116

commit v3 on v2

--- a/solution.py
+++ b/solution.py
@@ -10,6 +10,7 @@
 NS_STEPS = 5
 SPAN = 2
 LANES = 128
+PIECES = 4
 
 f32 = jnp.float32
 bf16 = jnp.bfloat16
@@ -55,17 +56,18 @@
         factor_out[block : block + 1, :] = jnp.where(chosen > 0.5, weight[...] * taper, 0.0)
 
 
-def gain_kernel(first, factor, gain_out):
-    members = first.shape[0]
-    blocks, rows = factor.shape
-    width = (first.shape[1] - rows) // blocks
-    values = first[:, :rows].astype(f32)
+def gain_kernel(pred, factor, gain_out, pred_buf, sem):
+    members, rows = pred.shape
+    load = pltpu.make_async_copy(pred, pred_buf, sem)
+    load.start()
+    load.wait()
+    values = pred_buf[...].astype(f32)
     deviation = values - jnp.mean(values, axis=0, keepdims=True)
     eye = (
         lax.broadcasted_iota(jnp.int32, (members, members), 0)
         == lax.broadcasted_iota(jnp.int32, (members, members), 1)
     ).astype(f32)
-    for block in range(blocks):
+    for block in range(factor.shape[0]):
         scaled = (factor[block : block + 1, :] * deviation * (1.0 / math.sqrt(members - 1.0))).astype(bf16)
         gram = contract_lanes(scaled, scaled)
         start = 2.0 / (2.0 + jnp.sqrt(jnp.sum(gram * gram)))
@@ -76,36 +78,61 @@
             residual = dot3(residual_parts, residual_parts)
             residual_parts = split(residual)
             estimate = estimate + dot3(split(estimate), residual_parts)
-        cells = first[:, rows + block * width : rows + (block + 1) * width].astype(f32)
+        high, low = split(estimate * (start * (1.0 / math.sqrt(members - 1.0))))
+        gain_out[:, block * members : (block + 1) * members] = (contract_rows(scaled, high) + contract_rows(scaled, low)).astype(bf16)
+
+
+def update_kernel(second, factor, pred, gain, updated, pred_buf, gain_buf, pred_sems, gain_sems):
+    blocks, rows = factor.shape
+    members = pred.shape[0]
+    width = (second.shape[1] - rows) // blocks
+    piece = rows // PIECES
+    pred_loads, gain_loads = [], []
+    for part in range(PIECES):
+        span = pl.ds(part * piece, piece)
+        pred_loads.append(pltpu.make_async_copy(pred.at[:, span], pred_buf.at[:, span], pred_sems.at[part]))
+        gain_loads.append(pltpu.make_async_copy(gain.at[span, :], gain_buf.at[span, :], gain_sems.at[part]))
+        pred_loads[part].start()
+        gain_loads[part].start()
+    weights_t = [None] * blocks
+    for part in range(PIECES):
+        span = slice(part * piece, (part + 1) * piece)
+        pred_loads[part].wait()
+        change = second[:, span].astype(f32) - pred_buf[:, span].astype(f32)
+        gain_loads[part].wait()
+        for block in range(blocks):
+            innovation = (factor[block : block + 1, span] * change).astype(bf16)
+            product = dot(innovation, gain_buf[span, block * members : (block + 1) * members])
+            weights_t[block] = product if part == 0 else weights_t[block] + product
+    for block in range(blocks):
+        span = slice(rows + block * width, rows + (block + 1) * width)
+        cells = second[:, span].astype(f32)
         centred = (cells - jnp.mean(cells, axis=0, keepdims=True)).astype(bf16)
-        high, low = split(estimate * (start * (1.0 / math.sqrt(members - 1.0))))
-        smoothed_high, smoothed_low = split(dot(high, centred) + dot(low, centred))
-        gain_out[block] = (
-            contract_rows(scaled, smoothed_high) + contract_rows(scaled, smoothed_low)
-        ).astype(bf16)
-
-
-def update_kernel(first, pert, factor, gain, updated):
-    blocks, rows = factor.shape
-    width = (first.shape[1] - rows) // blocks
-    change = pert[...].astype(f32) - first[:, :rows].astype(f32)
-    for block in range(blocks):
-        innovation = (factor[block : block + 1, :] * change).astype(bf16)
-        cells = first[:, rows + block * width : rows + (block + 1) * width].astype(f32)
-        updated[:, block * width : (block + 1) * width] = (cells + dot(innovation, gain[block])).astype(bf16)
-
-
-def call(kernel, outs, flops, scalars=0):
+        change = dot(weights_t[block].astype(bf16), centred)
+        updated[:, block * width : (block + 1) * width] = (cells + change).astype(bf16)
+
+
+def call(kernel, outs, flops, grant=None, scalars=0, stay=(), scratch=()):
     vmem = pl.BlockSpec(memory_space=pltpu.VMEM)
     smem = pl.BlockSpec(memory_space=pltpu.SMEM)
+    hbm = pl.BlockSpec(memory_space=pltpu.HBM)
 
     def run(*args):
+        specs = [smem] * scalars + [vmem] * (len(args) - scalars)
+        for place in stay:
+            specs[place] = hbm
+        args = [
+            pltpu.with_memory_space_constraint(arg, pltpu.HBM) if place in stay else arg
+            for place, arg in enumerate(args)
+        ]
         return pl.pallas_call(
             kernel,
             out_shape=outs,
-            in_specs=[smem] * scalars + [vmem] * (len(args) - scalars),
-            out_specs=jax.tree.map(lambda _: vmem, outs),
+            in_specs=specs,
+            out_specs=vmem,
+            scratch_shapes=list(scratch),
             cost_estimate=pl.CostEstimate(flops=flops, transcendentals=0, bytes_accessed=1 << 22),
+            compiler_params=pltpu.CompilerParams(vmem_limit_bytes=grant),
             name=kernel.__name__,
         )(*args)
 
@@ -125,11 +152,7 @@
     rows = predicted.shape[1] // groups
     cells = state.shape[1] // groups
 
-    paired = jnp.concatenate(
-        [predicted.reshape(held, groups, rows), state.reshape(held, groups, cells)], axis=2
-    )
-    first = exchange(paired)
-
+    pred_pool = exchange(predicted)
     counts = lax.dynamic_index_in_dim(row_count, tile_index, 0, keepdims=False)
     first_block = (tile_index * groups + group_index) * blocks
     scalars = jnp.concatenate([first_block[None].astype(jnp.int32), counts])
@@ -138,11 +161,32 @@
 
     shaped = jax.ShapeDtypeStruct
     cube = 2 * blocks * members**3
-    factor = call(factor_kernel, shaped((blocks, rows), f32), cube, 1)(scalars, row_index[0], weight, place)
-    factor, perturbed = lax.optimization_barrier((factor, perturbed))
-    pert_pool = exchange(perturbed)
-    gain = call(gain_kernel, shaped((blocks, rows, cells // blocks), bf16), 40 * cube)(first, factor)
-    updated = call(update_kernel, shaped((members, cells), bf16), 4 * cube)(first, pert_pool, factor, gain)
+    factor = call(factor_kernel, shaped((blocks, rows), f32), cube, 67043328, 1)(scalars, row_index[0], weight, place)
+    paired = jnp.concatenate(
+        [perturbed.reshape(held, groups, rows), state.reshape(held, groups, cells)], axis=2
+    )
+    factor, paired = lax.optimization_barrier((factor, paired))
+    second = exchange(paired)
+    gain = call(
+        gain_kernel,
+        shaped((rows, blocks * members), bf16),
+        40 * cube,
+        stay=(0,),
+        scratch=(pltpu.VMEM((members, rows), bf16), pltpu.SemaphoreType.DMA),
+    )(pred_pool, factor)
+    updated = call(
+        update_kernel,
+        shaped((members, cells), bf16),
+        5 * cube,
+        grant=24 << 20,
+        stay=(2, 3),
+        scratch=(
+            pltpu.VMEM((members, rows), bf16),
+            pltpu.VMEM(gain.shape, bf16),
+            pltpu.SemaphoreType.DMA((PIECES,)),
+            pltpu.SemaphoreType.DMA((PIECES,)),
+        ),
+    )(second, factor, pred_pool, gain)
     return lax.all_to_all(updated, "member", split_axis=0, concat_axis=1, tiled=True)
 
 

time: 129 us -> 122 us (0.946)
  waiting for transfers between devices: 38.8 us -> 35.5 us
  Pallas kernels: 36.5 us -> 33.9 us
    all_to_all x2, waiting for transfers between devices: 38.8 us -> 35.5 us  [per_device(): lax.all_to_all(value.reshape(value.shape[0], groups, -1), 'member', split...]
    pallas_call x3, Pallas kernels: 36.5 us -> 33.9 us  [run(): pl.pallas_call(kernel, out_shape=outs, in_specs=specs, out_specs=vmem, sc...]
  transfers between devices with their start and end apart: 2 -> 2, of which waited for: 2 -> 2; matrix products, arithmetic and copies ran while one was open for 2% -> 6% of each run, Pallas kernels for 23% -> 23%
where the time goes in v3:
time: 122 us; the launch traced here: 121 us
  waiting for transfers between devices  35.5 us (29%)
  Pallas kernels  33.9 us (28%)
  blocking collectives  25.8 us (21%)
  starting transfers between devices  17.9 us (15%)
  other arithmetic  4.44 us (4%)
  local copies, waits for them, and re-layouts  3.58 us (3%)
    all_to_all x2, waiting for transfers between devices, per_device(): lax.all_to_all(value.reshape(value.shape[0], groups, -1), 'member', split...  35.5 us
    pallas_call x3, Pallas kernels, run(): pl.pallas_call(kernel, out_shape=outs, in_specs=specs, out_specs=vmem, sc...  33.9 us
    all_to_all x1, blocking collectives, per_device(): lax.all_to_all(updated, 'member', split_axis=0, concat_axis=1, tiled=True)  25.8 us
    all_to_all x2, starting transfers between devices, per_device(): lax.all_to_all(value.reshape(value.shape[0], groups, -1), 'member', split...  17.9 us
    concatenate x1, other arithmetic, per_device(): jnp.concatenate([perturbed.reshape(held, groups, rows), state.reshape(hel...  3.86 us
  transfers between devices with their start and end apart: 2, of which 2 were waited for; matrix products, arithmetic and copies ran while one was open for 6% of the time, Pallas kernels for 23%

profile of v3, /device:TPU:0, one launch (start us, length us, event | category | flops | bytes accessed | tf_op | source)
XLA Modules:
  0.0 121.2 jit_solution(8778020055192861977)
XLA Ops:
  0.0 0.0 copy-start.1
  0.0 11.9 %all-to-all-start.1 = ((bf16[8,64,2048]{2,0,1:T(8,128)(2,1)}), bf16[8,64,2048]{2,0,1:T(8,128)(2,1)}, u32[]{:S(2)}, u32[]{:S(2)}) async-start(bf16[8,64,2048]{2,0,1:T(8,128)(2,1)} %bitcast.27), calls=%async_computation.1 | async-start | bytes 4194304 | tf_op jit(solution)/shard_map/all_to_all | solution.py:143
  11.9 1.3 %dynamic_slice.11 = f32[2048]{0:T(1024)} dynamic-slice(f32[131072]{0:T(1024)} %param.10, s32[]{:T(128)S(6)} %select_n.9), dynamic_slice_sizes={2048} | dynamic-slice | bytes 16388 | tf_op jit(solution)/shard_map/dynamic_slice | solution.py:159
  13.2 1.3 %dynamic_slice.12 = s32[2048]{0:T(1024)} dynamic-slice(s32[131072]{0:T(1024)} %param.11, s32[]{:T(128)S(6)} %select_n.9), dynamic_slice_sizes={2048} | dynamic-slice | bytes 16388 | tf_op jit(solution)/shard_map/dynamic_slice | solution.py:160
  14.5 0.0 copy-done.1
  14.6 0.6 pad_add_fusion.scalars
  15.1 1.8 %factor_kernel.1.factor = f32[2,2048]{1,0:T(2,128)} custom-call(s32[3]{0:T(128)} %pad_add_fusion.scalars, s32[2,2048]{1,0:T(2,128)} %bitcast.31, f32[1,2048]{1,0:T(1,128)} %bitcast.29, s32[1,2048]{1,0:T(1,128)} %bitcast.30), custom_call_target="tpu_custom_call" | custom-call | flops 536870912 | bytes 4194304 | tf_op jit(solution)/shard_map/factor_kernel/pallas_call | solution.py:128
  17.0 3.9 %pad_maximum_fusion = bf16[8,64,3072]{2,0,1:T(8,128)(2,1)} fusion(bf16[8,64,1024]{2,0,1:T(8,128)(2,1)} %bitcast.28, bf16[8,64,2048]{2,0,1:T(8,128)(2,1)} %bitcast.26), kind=kLoop, calls=%fused_computation | loop fusion | flops 6291456 | bytes 6291456 | tf_op jit(solution)/shard_map/concatenate | solution.py:165
  20.8 20.9 %all-to-all-done.1 = bf16[8,64,2048]{2,0,1:T(8,128)(2,1)} async-done(((bf16[8,64,2048]{2,0,1:T(8,128)(2,1)}), bf16[8,64,2048]{2,0,1:T(8,128)(2,1)}, u32[]{:S(2)}, u32[]{:S(2)}) %all-to-all-start.1) | async-done | bytes 2097184 | tf_op jit(solution)/shard_map/all_to_all | solution.py:143
  41.7 6.0 %all-to-all-start = ((bf16[8,64,3072]{2,0,1:T(8,128)(2,1)}), bf16[8,64,3072]{2,0,1:T(8,128)(2,1)S(1)}, u32[]{:S(2)}, u32[]{:S(2)}) async-start(bf16[8,64,3072]{2,0,1:T(8,128)(2,1)} %pad_maximum_fusion), calls=%async_computation | async-start | bytes 6291456 | tf_op jit(solution)/shard_map/all_to_all | solution.py:143
  47.8 0.0 copy-start
  47.8 26.7 %gain_kernel.1.gain = bf16[2048,1024]{1,0:T(8,128)(2,1)} custom-call(bf16[512,2048]{1,0:T(8,128)(2,1)} %bitcast.13.pred, f32[2,2048]{1,0:T(2,128)} %factor_kernel.1.factor), custom_call_target="tpu_custom_call" | custom-call | flops 21474836480 | bytes 4194304 | tf_op jit(solution)/shard_map/gain_kernel/pallas_call | solution.py:128
  74.5 14.6 %all-to-all-done = bf16[8,64,3072]{2,0,1:T(8,128)(2,1)S(1)} async-done(((bf16[8,64,3072]{2,0,1:T(8,128)(2,1)}), bf16[8,64,3072]{2,0,1:T(8,128)(2,1)S(1)}, u32[]{:S(2)}, u32[]{:S(2)}) %all-to-all-start) | async-done | bytes 3145760 | tf_op jit(solution)/shard_map/all_to_all | solution.py:143
  89.0 0.0 copy-done
  89.0 5.4 %update_kernel.1 = bf16[512,1024]{1,0:T(8,128)(2,1)S(1)} custom-call(bf16[512,3072]{1,0:T(8,128)(2,1)S(1)} %bitcast.23, f32[2,2048]{1,0:T(2,128)S(1)} %copy-done, bf16[512,2048]{1,0:T(8,128)(2,1)} %bitcast.13.pred, bf16[2048,1024]{1,0:T(8,128)(2,1)} %gain_kernel.1.gain), custom_call_target="tpu_custom_call" | custom-call | flops 2684354560 | bytes 4194304 | tf_op jit(solution)/shard_map/update_kernel/pallas_call | solution.py:128
  94.4 25.8 %all_to_all.49 = bf16[64,8,1024]{2,1,0:T(8,128)(2,1)S(1)} all-to-all(bf16[64,8,1024]{2,1,0:T(8,128)(2,1)S(1)} %bitcast.24), channel_id=1, replica_groups=mesh['member'=64,'domain'=2] {'member'}, dimensions={0} | all-to-all | bytes 2097152 | tf_op jit(solution)/shard_map/all_to_all | solution.py:190
  120.2 1.0 copy.9
  (1 shorter events, 0.0 us)
Async XLA Ops:
  0.0 14.5 %copy-start.1 = (s32[2,2]{1,0:T(2,128)S(1)}, s32[2,2]{1,0:T(2,128)}, u32[]{:S(2)}) copy-start(s32[2,2]{1,0:T(2,128)} %param.12) | copy-start | bytes 52
  0.0 41.7 %all-to-all-start.1 = ((bf16[8,64,2048]{2,0,1:T(8,128)(2,1)}), bf16[8,64,2048]{2,0,1:T(8,128)(2,1)}, u32[]{:S(2)}, u32[]{:S(2)}) async-start(bf16[8,64,2048]{2,0,1:T(8,128)(2,1)} %bitcast.27), calls=%async_computation.1 | async-start | bytes 4194304 | tf_op jit(solution)/shard_map/all_to_all | solution.py:143
  41.7 47.3 %all-to-all-start = ((bf16[8,64,3072]{2,0,1:T(8,128)(2,1)}), bf16[8,64,3072]{2,0,1:T(8,128)(2,1)S(1)}, u32[]{:S(2)}, u32[]{:S(2)}) async-start(bf16[8,64,3072]{2,0,1:T(8,128)(2,1)} %pad_maximum_fusion), calls=%async_computation | async-start | bytes 6291456 | tf_op jit(solution)/shard_map/all_to_all | solution.py:143
  47.8 41.3 %copy-start = (f32[2,2048]{1,0:T(2,128)S(1)}, f32[2,2048]{1,0:T(2,128)}, u32[]{:S(2)}) copy-start(f32[2,2048]{1,0:T(2,128)} %factor_kernel.1.factor) | copy-start | bytes 49156

commit v4 on v3

--- a/solution.py
+++ b/solution.py
@@ -11,6 +11,7 @@
 SPAN = 2
 LANES = 128
 PIECES = 4
+HELD = 8
 
 f32 = jnp.float32
 bf16 = jnp.bfloat16
@@ -108,8 +109,9 @@
         span = slice(rows + block * width, rows + (block + 1) * width)
         cells = second[:, span].astype(f32)
         centred = (cells - jnp.mean(cells, axis=0, keepdims=True)).astype(bf16)
-        change = dot(weights_t[block].astype(bf16), centred)
-        updated[:, block * width : (block + 1) * width] = (cells + change).astype(bf16)
+        total = cells + dot(weights_t[block].astype(bf16), centred)
+        total = jnp.concatenate([total[row : row + HELD] for row in range(members - HELD, -1, -HELD)], axis=0)
+        updated[:, block * width : (block + 1) * width] = total.astype(bf16)
 
 
 def call(kernel, outs, flops, grant=None, scalars=0, stay=(), scratch=()):
@@ -187,7 +189,11 @@
             pltpu.SemaphoreType.DMA((PIECES,)),
         ),
     )(second, factor, pred_pool, gain)
-    return lax.all_to_all(updated, "member", split_axis=0, concat_axis=1, tiled=True)
+    backwards = [list(range(groups))[::-1]]
+    returned = lax.all_to_all(
+        updated, "member", split_axis=0, concat_axis=1, tiled=True, axis_index_groups=backwards
+    )
+    return jnp.flip(returned.reshape(held, groups, cells), axis=1).reshape(held, -1)
 
 
 def solution(mesh):

time: 122 us -> 117 us (0.959)
  blocking collectives: 25.8 us -> 20.9 us
    all_to_all x1, blocking collectives: 25.8 us -> 20.9 us  [per_device(): lax.all_to_all(updated, 'member', split_axis=0, concat_axis=1, tiled=True...]
  transfers between devices with their start and end apart: 2 -> 2, of which waited for: 2 -> 2; matrix products, arithmetic and copies ran while one was open for 6% -> 6% of each run, Pallas kernels for 23% -> 24%
where the time goes in v4:
time: 117 us; the launch traced here: 116 us
  waiting for transfers between devices  35.5 us (30%)
  Pallas kernels  33.9 us (29%)
  blocking collectives  20.9 us (18%)
  starting transfers between devices  17.9 us (15%)
  other arithmetic  4.44 us (4%)
  local copies, waits for them, and re-layouts  3.65 us (3%)
    all_to_all x2, waiting for transfers between devices, per_device(): lax.all_to_all(value.reshape(value.shape[0], groups, -1), 'member', split...  35.5 us
    pallas_call x3, Pallas kernels, run(): pl.pallas_call(kernel, out_shape=outs, in_specs=specs, out_specs=vmem, sc...  33.9 us
    all_to_all x1, blocking collectives, per_device(): lax.all_to_all(updated, 'member', split_axis=0, concat_axis=1, tiled=True...  20.9 us
    all_to_all x2, starting transfers between devices, per_device(): lax.all_to_all(value.reshape(value.shape[0], groups, -1), 'member', split...  17.9 us
    concatenate x1, other arithmetic, per_device(): jnp.concatenate([perturbed.reshape(held, groups, rows), state.reshape(hel...  3.86 us
  transfers between devices with their start and end apart: 2, of which 2 were waited for; matrix products, arithmetic and copies ran while one was open for 6% of the time, Pallas kernels for 24%

profile of v4, /device:TPU:0, one launch (start us, length us, event | category | flops | bytes accessed | tf_op | source)
XLA Modules:
  0.0 116.4 jit_solution(17179175571473195324)
XLA Ops:
  0.0 0.0 copy-start.1
  0.0 11.9 %all-to-all-start.1 = ((bf16[8,64,2048]{2,0,1:T(8,128)(2,1)}), bf16[8,64,2048]{2,0,1:T(8,128)(2,1)}, u32[]{:S(2)}, u32[]{:S(2)}) async-start(bf16[8,64,2048]{2,0,1:T(8,128)(2,1)} %bitcast.26), calls=%async_computation.1 | async-start | bytes 4194304 | tf_op jit(solution)/shard_map/all_to_all | solution.py:145
  11.9 1.3 %dynamic_slice.11 = f32[2048]{0:T(1024)} dynamic-slice(f32[131072]{0:T(1024)} %param.10, s32[]{:T(128)S(6)} %select_n.9), dynamic_slice_sizes={2048} | dynamic-slice | bytes 16388 | tf_op jit(solution)/shard_map/dynamic_slice | solution.py:161
  13.2 1.3 %dynamic_slice.12 = s32[2048]{0:T(1024)} dynamic-slice(s32[131072]{0:T(1024)} %param.11, s32[]{:T(128)S(6)} %select_n.9), dynamic_slice_sizes={2048} | dynamic-slice | bytes 16388 | tf_op jit(solution)/shard_map/dynamic_slice | solution.py:162
  14.5 0.0 copy-done.1
  14.6 0.6 pad_add_fusion.scalars
  15.1 1.8 %factor_kernel.1.factor = f32[2,2048]{1,0:T(2,128)} custom-call(s32[3]{0:T(128)} %pad_add_fusion.scalars, s32[2,2048]{1,0:T(2,128)} %bitcast.30, f32[1,2048]{1,0:T(1,128)} %bitcast.28, s32[1,2048]{1,0:T(1,128)} %bitcast.29), custom_call_target="tpu_custom_call" | custom-call | flops 536870912 | bytes 4194304 | tf_op jit(solution)/shard_map/factor_kernel/pallas_call | solution.py:130
  17.0 3.9 %pad_maximum_fusion = bf16[8,64,3072]{2,0,1:T(8,128)(2,1)} fusion(bf16[8,64,1024]{2,0,1:T(8,128)(2,1)} %bitcast.27, bf16[8,64,2048]{2,0,1:T(8,128)(2,1)} %bitcast.25), kind=kLoop, calls=%fused_computation | loop fusion | flops 6291456 | bytes 6291456 | tf_op jit(solution)/shard_map/concatenate | solution.py:167
  20.8 20.9 %all-to-all-done.1 = bf16[8,64,2048]{2,0,1:T(8,128)(2,1)} async-done(((bf16[8,64,2048]{2,0,1:T(8,128)(2,1)}), bf16[8,64,2048]{2,0,1:T(8,128)(2,1)}, u32[]{:S(2)}, u32[]{:S(2)}) %all-to-all-start.1) | async-done | bytes 2097184 | tf_op jit(solution)/shard_map/all_to_all | solution.py:145
  41.7 6.0 %all-to-all-start = ((bf16[8,64,3072]{2,0,1:T(8,128)(2,1)}), bf16[8,64,3072]{2,0,1:T(8,128)(2,1)S(1)}, u32[]{:S(2)}, u32[]{:S(2)}) async-start(bf16[8,64,3072]{2,0,1:T(8,128)(2,1)} %pad_maximum_fusion), calls=%async_computation | async-start | bytes 6291456 | tf_op jit(solution)/shard_map/all_to_all | solution.py:145
  47.8 0.0 copy-start
  47.8 26.7 %gain_kernel.1.gain = bf16[2048,1024]{1,0:T(8,128)(2,1)} custom-call(bf16[512,2048]{1,0:T(8,128)(2,1)} %bitcast.13.pred, f32[2,2048]{1,0:T(2,128)} %factor_kernel.1.factor), custom_call_target="tpu_custom_call" | custom-call | flops 21474836480 | bytes 4194304 | tf_op jit(solution)/shard_map/gain_kernel/pallas_call | solution.py:130
  74.5 14.6 %all-to-all-done = bf16[8,64,3072]{2,0,1:T(8,128)(2,1)S(1)} async-done(((bf16[8,64,3072]{2,0,1:T(8,128)(2,1)}), bf16[8,64,3072]{2,0,1:T(8,128)(2,1)S(1)}, u32[]{:S(2)}, u32[]{:S(2)}) %all-to-all-start) | async-done | bytes 3145760 | tf_op jit(solution)/shard_map/all_to_all | solution.py:145
  89.0 0.0 copy-done
  89.0 5.4 %update_kernel.1 = bf16[512,1024]{1,0:T(8,128)(2,1)S(1)} custom-call(bf16[512,3072]{1,0:T(8,128)(2,1)S(1)} %bitcast.22, f32[2,2048]{1,0:T(2,128)S(1)} %copy-done, bf16[512,2048]{1,0:T(8,128)(2,1)} %bitcast.13.pred, bf16[2048,1024]{1,0:T(8,128)(2,1)} %gain_kernel.1.gain), custom_call_target="tpu_custom_call" | custom-call | flops 2684354560 | bytes 4194304 | tf_op jit(solution)/shard_map/update_kernel/pallas_call | solution.py:130
  94.4 20.9 %all_to_all.46 = bf16[64,8,1024]{2,1,0:T(8,128)(2,1)S(1)} all-to-all(bf16[64,8,1024]{2,1,0:T(8,128)(2,1)S(1)} %bitcast.23), channel_id=1, replica_groups={{126,124,122,120,118,116,114,112,110,108,106,104,102,100,98,96,94,92,90..., dimensions={0} | all-to-all | bytes 2097152 | tf_op jit(solution)/shard_map/all_to_all | solution.py:193
  115.4 1.0 reverse.3
  (1 shorter events, 0.0 us)
Async XLA Ops:
  0.0 14.5 %copy-start.1 = (s32[2,2]{1,0:T(2,128)S(1)}, s32[2,2]{1,0:T(2,128)}, u32[]{:S(2)}) copy-start(s32[2,2]{1,0:T(2,128)} %param.12) | copy-start | bytes 52
  0.0 41.7 %all-to-all-start.1 = ((bf16[8,64,2048]{2,0,1:T(8,128)(2,1)}), bf16[8,64,2048]{2,0,1:T(8,128)(2,1)}, u32[]{:S(2)}, u32[]{:S(2)}) async-start(bf16[8,64,2048]{2,0,1:T(8,128)(2,1)} %bitcast.26), calls=%async_computation.1 | async-start | bytes 4194304 | tf_op jit(solution)/shard_map/all_to_all | solution.py:145
  41.7 47.3 %all-to-all-start = ((bf16[8,64,3072]{2,0,1:T(8,128)(2,1)}), bf16[8,64,3072]{2,0,1:T(8,128)(2,1)S(1)}, u32[]{:S(2)}, u32[]{:S(2)}) async-start(bf16[8,64,3072]{2,0,1:T(8,128)(2,1)} %pad_maximum_fusion), calls=%async_computation | async-start | bytes 6291456 | tf_op jit(solution)/shard_map/all_to_all | solution.py:145
  47.8 41.3 %copy-start = (f32[2,2048]{1,0:T(2,128)S(1)}, f32[2,2048]{1,0:T(2,128)}, u32[]{:S(2)}) copy-start(f32[2,2048]{1,0:T(2,128)} %factor_kernel.1.factor) | copy-start | bytes 49156

commit v5 on v3

--- a/solution.py
+++ b/solution.py
@@ -11,6 +11,7 @@
 SPAN = 2
 LANES = 128
 PIECES = 4
+HELD = 8
 
 f32 = jnp.float32
 bf16 = jnp.bfloat16
@@ -37,6 +38,11 @@
     left_high, left_low = left
     right_high, right_low = right
     return dot(left_high, right_high) + (dot(left_high, right_low) + dot(left_low, right_high))
+
+
+def backwards(value):
+    last = value.shape[0] - HELD
+    return jnp.concatenate([value[row : row + HELD] for row in range(last, -1, -HELD)], axis=0)
 
 
 def factor_kernel(scalars, index, weight, place, factor_out):
@@ -61,7 +67,7 @@
     load = pltpu.make_async_copy(pred, pred_buf, sem)
     load.start()
     load.wait()
-    values = pred_buf[...].astype(f32)
+    values = backwards(pred_buf[...].astype(f32))
     deviation = values - jnp.mean(values, axis=0, keepdims=True)
     eye = (
         lax.broadcasted_iota(jnp.int32, (members, members), 0)
@@ -98,7 +104,7 @@
     for part in range(PIECES):
         span = slice(part * piece, (part + 1) * piece)
         pred_loads[part].wait()
-        change = second[:, span].astype(f32) - pred_buf[:, span].astype(f32)
+        change = second[:, span].astype(f32) - backwards(pred_buf[:, span].astype(f32))
         gain_loads[part].wait()
         for block in range(blocks):
             innovation = (factor[block : block + 1, span] * change).astype(bf16)
@@ -140,9 +146,13 @@
 
 
 def per_device(state, predicted, perturbed, obs_weight, obs_position, row_count, row_index):
-    exchange = lambda value: lax.all_to_all(
-        value.reshape(value.shape[0], groups, -1), "member", split_axis=1, concat_axis=0, tiled=True
-    ).reshape(members, -1)
+    def exchange(value, order=None):
+        chunks = value.reshape(held, groups, -1)
+        received = lax.all_to_all(
+            chunks, "member", split_axis=1, concat_axis=0, tiled=True, axis_index_groups=order
+        )
+        return received.reshape(members, -1)
+
     groups = lax.axis_size("member")
     group_index = lax.axis_index("member")
     tile_index = lax.axis_index("domain")
@@ -151,6 +161,7 @@
     members = held * groups
     rows = predicted.shape[1] // groups
     cells = state.shape[1] // groups
+    from_last = [list(range(groups))[::-1]]
 
     pred_pool = exchange(predicted)
     counts = lax.dynamic_index_in_dim(row_count, tile_index, 0, keepdims=False)
@@ -165,8 +176,8 @@
     paired = jnp.concatenate(
         [perturbed.reshape(held, groups, rows), state.reshape(held, groups, cells)], axis=2
     )
-    factor, paired = lax.optimization_barrier((factor, paired))
-    second = exchange(paired)
+    factor, paired = lax.optimization_barrier((factor, jnp.flip(paired, axis=1)))
+    second = exchange(paired, from_last)
     gain = call(
         gain_kernel,
         shaped((rows, blocks * members), bf16),
@@ -187,7 +198,10 @@
             pltpu.SemaphoreType.DMA((PIECES,)),
         ),
     )(second, factor, pred_pool, gain)
-    return lax.all_to_all(updated, "member", split_axis=0, concat_axis=1, tiled=True)
+    returned = lax.all_to_all(
+        updated, "member", split_axis=0, concat_axis=1, tiled=True, axis_index_groups=from_last
+    )
+    return jnp.flip(returned.reshape(held, groups, cells), axis=1).reshape(held, -1)
 
 
 def solution(mesh):

time: 122 us -> 117 us (0.959)
  waiting for transfers between devices: 35.5 us -> 27.7 us
  starting transfers between devices: 17.9 us -> 21.6 us
  local copies, waits for them, and re-layouts: 3.58 us -> 5.54 us
  other arithmetic: 4.44 us -> 2.76 us
    all_to_all x2, waiting for transfers between devices: 35.5 us -> 27.7 us  [exchange(): lax.all_to_all(chunks, 'member', split_axis=1, concat_axis=0, tiled=True,...]
    all_to_all x2, starting transfers between devices: 17.9 us -> 21.6 us  [exchange(): lax.all_to_all(chunks, 'member', split_axis=1, concat_axis=0, tiled=True,...]
    rev x0 -> x1, local copies, waits for them, and re-layouts: none -> 1.89 us  [per_device(): jnp.flip(paired, axis=1)]
    concatenate x1, other arithmetic: 3.86 us -> 2.18 us  [per_device(): jnp.concatenate([perturbed.reshape(held, groups, rows), state.reshape(hel...]
  transfers between devices with their start and end apart: 2 -> 2, of which waited for: 2 -> 2; matrix products, arithmetic and copies ran while one was open for 6% -> 6% of each run, Pallas kernels for 23% -> 24%
where the time goes in v5:
time: 117 us
  Pallas kernels  33.8 us (29%)
  waiting for transfers between devices  27.7 us (24%)
  blocking collectives  25.2 us (22%)
  starting transfers between devices  21.6 us (18%)
  local copies, waits for them, and re-layouts  5.54 us (5%)
  other arithmetic  2.76 us (2%)
    pallas_call x3, Pallas kernels, run(): pl.pallas_call(kernel, out_shape=outs, in_specs=specs, out_specs=vmem, sc...  33.8 us
    all_to_all x2, waiting for transfers between devices, exchange(): lax.all_to_all(chunks, 'member', split_axis=1, concat_axis=0, tiled=True,...  27.7 us
    all_to_all x1, blocking collectives, per_device(): lax.all_to_all(updated, 'member', split_axis=0, concat_axis=1, tiled=True...  25.2 us
    all_to_all x2, starting transfers between devices, exchange(): lax.all_to_all(chunks, 'member', split_axis=1, concat_axis=0, tiled=True,...  21.6 us
  transfers between devices with their start and end apart: 2, of which 2 were waited for; matrix products, arithmetic and copies ran while one was open for 6% of the time, Pallas kernels for 24%

profile of v5, /device:TPU:0, one launch (start us, length us, event | category | flops | bytes accessed | tf_op | source)
XLA Modules:
  0.0 116.7 jit_solution(10170104547612818412)
XLA Ops:
  0.0 11.8 %all-to-all-start.1 = ((bf16[8,64,2048]{2,0,1:T(8,128)(2,1)}), bf16[8,64,2048]{2,0,1:T(8,128)(2,1)}, u32[]{:S(2)}, u32[]{:S(2)}) async-start(bf16[8,64,2048]{2,0,1:T(8,128)(2,1)} %bitcast.26), calls=%async_computation.1 | async-start | bytes 4194304 | tf_op jit(solution)/shard_map/all_to_all | solution.py:151
  11.8 1.3 %dynamic_slice.11 = f32[2048]{0:T(1024)} dynamic-slice(f32[131072]{0:T(1024)} %param.10, s32[]{:T(128)S(6)} %select_n.9), dynamic_slice_sizes={2048} | dynamic-slice | bytes 16388 | tf_op jit(solution)/shard_map/dynamic_slice | solution.py:170
  13.1 1.3 %dynamic_slice.12 = s32[2048]{0:T(1024)} dynamic-slice(s32[131072]{0:T(1024)} %param.11, s32[]{:T(128)S(6)} %select_n.9), dynamic_slice_sizes={2048} | dynamic-slice | bytes 16388 | tf_op jit(solution)/shard_map/dynamic_slice | solution.py:171
  14.4 2.2 %pad_maximum_fusion = bf16[8,64,3072]{2,0,1:T(8,128)(2,1)S(1)} fusion(bf16[8,64,1024]{2,0,1:T(8,128)(2,1)} %bitcast.27, bf16[8,64,2048]{2,0,1:T(8,128)(2,1)} %bitcast.25), kind=kLoop, calls=%fused_computation | loop fusion | flops 6291456 | bytes 6291456 | tf_op jit(solution)/shard_map/concatenate | solution.py:176
  16.6 0.0 copy-start.1
  16.6 1.9 %rev.6 = bf16[8,64,3072]{2,0,1:T(8,128)(2,1)} reverse(bf16[8,64,3072]{2,0,1:T(8,128)(2,1)S(1)} %pad_maximum_fusion), dimensions={1} | reverse | bytes 6291456 | tf_op jit(solution)/shard_map/jit(_flip)/rev | solution.py:179
  18.5 0.0 copy-done.1
  18.5 0.6 pad_add_fusion.scalars
  19.1 1.8 %factor_kernel.1.factor = f32[2,2048]{1,0:T(2,128)} custom-call(s32[3]{0:T(128)} %pad_add_fusion.scalars, s32[2,2048]{1,0:T(2,128)} %bitcast.30, f32[1,2048]{1,0:T(1,128)} %bitcast.28, s32[1,2048]{1,0:T(1,128)} %bitcast.29), custom_call_target="tpu_custom_call" | custom-call | flops 536870912 | bytes 4194304 | tf_op jit(solution)/shard_map/factor_kernel/pallas_call | solution.py:134
  20.9 20.7 %all-to-all-done.1 = bf16[8,64,2048]{2,0,1:T(8,128)(2,1)} async-done(((bf16[8,64,2048]{2,0,1:T(8,128)(2,1)}), bf16[8,64,2048]{2,0,1:T(8,128)(2,1)}, u32[]{:S(2)}, u32[]{:S(2)}) %all-to-all-start.1) | async-done | bytes 2097184 | tf_op jit(solution)/shard_map/all_to_all | solution.py:151
  41.6 9.8 %all-to-all-start = ((bf16[8,64,3072]{2,0,1:T(8,128)(2,1)}), bf16[8,64,3072]{2,0,1:T(8,128)(2,1)S(1)}, u32[]{:S(2)}, u32[]{:S(2)}) async-start(bf16[8,64,3072]{2,0,1:T(8,128)(2,1)} %rev.6), calls=%async_computation | async-start | bytes 6291456 | tf_op jit(solution)/shard_map/all_to_all | solution.py:151
  51.4 0.0 copy-start
  51.4 26.7 %gain_kernel.1.gain = bf16[2048,1024]{1,0:T(8,128)(2,1)} custom-call(bf16[512,2048]{1,0:T(8,128)(2,1)} %bitcast.13.pred, f32[2,2048]{1,0:T(2,128)} %factor_kernel.1.factor), custom_call_target="tpu_custom_call" | custom-call | flops 21474836480 | bytes 4194304 | tf_op jit(solution)/shard_map/gain_kernel/pallas_call | solution.py:134
  78.1 7.0 %all-to-all-done = bf16[8,64,3072]{2,0,1:T(8,128)(2,1)S(1)} async-done(((bf16[8,64,3072]{2,0,1:T(8,128)(2,1)}), bf16[8,64,3072]{2,0,1:T(8,128)(2,1)S(1)}, u32[]{:S(2)}, u32[]{:S(2)}) %all-to-all-start) | async-done | bytes 3145760 | tf_op jit(solution)/shard_map/all_to_all | solution.py:151
  85.1 0.0 copy-done
  85.1 5.4 %update_kernel.1 = bf16[512,1024]{1,0:T(8,128)(2,1)S(1)} custom-call(bf16[512,3072]{1,0:T(8,128)(2,1)S(1)} %bitcast.22, f32[2,2048]{1,0:T(2,128)S(1)} %copy-done, bf16[512,2048]{1,0:T(8,128)(2,1)} %bitcast.13.pred, bf16[2048,1024]{1,0:T(8,128)(2,1)} %gain_kernel.1.gain), custom_call_target="tpu_custom_call" | custom-call | flops 2684354560 | bytes 4194304 | tf_op jit(solution)/shard_map/update_kernel/pallas_call | solution.py:134
  90.5 25.2 %all_to_all.46 = bf16[64,8,1024]{2,1,0:T(8,128)(2,1)S(1)} all-to-all(bf16[64,8,1024]{2,1,0:T(8,128)(2,1)S(1)} %bitcast.23), channel_id=1, replica_groups={{126,124,122,120,118,116,114,112,110,108,106,104,102,100,98,96,94,92,90..., dimensions={0} | all-to-all | bytes 2097152 | tf_op jit(solution)/shard_map/all_to_all | solution.py:201
  115.7 1.0 reverse.3
  (1 shorter events, 0.0 us)
Async XLA Ops:
  0.0 41.6 %all-to-all-start.1 = ((bf16[8,64,2048]{2,0,1:T(8,128)(2,1)}), bf16[8,64,2048]{2,0,1:T(8,128)(2,1)}, u32[]{:S(2)}, u32[]{:S(2)}) async-start(bf16[8,64,2048]{2,0,1:T(8,128)(2,1)} %bitcast.26), calls=%async_computation.1 | async-start | bytes 4194304 | tf_op jit(solution)/shard_map/all_to_all | solution.py:151
  16.6 1.9 %copy-start.1 = (s32[2,2]{1,0:T(2,128)S(1)}, s32[2,2]{1,0:T(2,128)}, u32[]{:S(2)}) copy-start(s32[2,2]{1,0:T(2,128)} %param.12) | copy-start | bytes 52
  41.6 43.5 %all-to-all-start = ((bf16[8,64,3072]{2,0,1:T(8,128)(2,1)}), bf16[8,64,3072]{2,0,1:T(8,128)(2,1)S(1)}, u32[]{:S(2)}, u32[]{:S(2)}) async-start(bf16[8,64,3072]{2,0,1:T(8,128)(2,1)} %rev.6), calls=%async_computation | async-start | bytes 6291456 | tf_op jit(solution)/shard_map/all_to_all | solution.py:151
  51.4 33.7 %copy-start = (f32[2,2048]{1,0:T(2,128)S(1)}, f32[2,2048]{1,0:T(2,128)}, u32[]{:S(2)}) copy-start(f32[2,2048]{1,0:T(2,128)} %factor_kernel.1.factor) | copy-start | bytes 49156

commit v6 on v5

--- a/solution.py
+++ b/solution.py
@@ -43,6 +43,12 @@
 def backwards(value):
     last = value.shape[0] - HELD
     return jnp.concatenate([value[row : row + HELD] for row in range(last, -1, -HELD)], axis=0)
+
+
+def from_middle(value):
+    groups = value.shape[0] // HELD
+    order = [groups - 1 - (groups // 2 + spot) % groups for spot in range(groups)]
+    return jnp.concatenate([value[spot * HELD : (spot + 1) * HELD] for spot in order], axis=0)
 
 
 def factor_kernel(scalars, index, weight, place, factor_out):
@@ -114,8 +120,8 @@
         span = slice(rows + block * width, rows + (block + 1) * width)
         cells = second[:, span].astype(f32)
         centred = (cells - jnp.mean(cells, axis=0, keepdims=True)).astype(bf16)
-        change = dot(weights_t[block].astype(bf16), centred)
-        updated[:, block * width : (block + 1) * width] = (cells + change).astype(bf16)
+        total = from_middle(cells + dot(weights_t[block].astype(bf16), centred))
+        updated[:, block * width : (block + 1) * width] = total.astype(bf16)
 
 
 def call(kernel, outs, flops, grant=None, scalars=0, stay=(), scratch=()):
@@ -198,10 +204,12 @@
             pltpu.SemaphoreType.DMA((PIECES,)),
         ),
     )(second, factor, pred_pool, gain)
+    half = groups // 2
+    middle_first = [[(half + spot) % groups for spot in range(groups)]]
     returned = lax.all_to_all(
-        updated, "member", split_axis=0, concat_axis=1, tiled=True, axis_index_groups=from_last
-    )
-    return jnp.flip(returned.reshape(held, groups, cells), axis=1).reshape(held, -1)
+        updated, "member", split_axis=0, concat_axis=1, tiled=True, axis_index_groups=middle_first
+    )
+    return jnp.flip(returned.reshape(held, 2, half * cells), axis=1).reshape(held, -1)
 
 
 def solution(mesh):

time: 117 us -> 116 us (level)
  blocking collectives: 25.2 us -> 23.9 us
    all_to_all x1, blocking collectives: 25.2 us -> 23.9 us  [per_device(): lax.all_to_all(updated, 'member', split_axis=0, concat_axis=1, tiled=True...]
  transfers between devices with their start and end apart: 2 -> 2, of which waited for: 2 -> 2; matrix products, arithmetic and copies ran while one was open for 6% -> 6% of each run, Pallas kernels for 24% -> 25%
where the time goes in v6:
time: 116 us; the launch traced here: 115 us
  Pallas kernels  33.8 us (29%)
  waiting for transfers between devices  27.7 us (24%)
  blocking collectives  23.9 us (21%)
  starting transfers between devices  21.6 us (19%)
  local copies, waits for them, and re-layouts  5.54 us (5%)
  other arithmetic  2.76 us (2%)
    pallas_call x3, Pallas kernels, run(): pl.pallas_call(kernel, out_shape=outs, in_specs=specs, out_specs=vmem, sc...  33.8 us
    all_to_all x2, waiting for transfers between devices, exchange(): lax.all_to_all(chunks, 'member', split_axis=1, concat_axis=0, tiled=True,...  27.7 us
    all_to_all x1, blocking collectives, per_device(): lax.all_to_all(updated, 'member', split_axis=0, concat_axis=1, tiled=True...  23.9 us
    all_to_all x2, starting transfers between devices, exchange(): lax.all_to_all(chunks, 'member', split_axis=1, concat_axis=0, tiled=True,...  21.6 us
  transfers between devices with their start and end apart: 2, of which 2 were waited for; matrix products, arithmetic and copies ran while one was open for 6% of the time, Pallas kernels for 25%

profile of v6, /device:TPU:0, one launch (start us, length us, event | category | flops | bytes accessed | tf_op | source)
XLA Modules:
  0.0 115.4 jit_solution(18119495429347180783)
XLA Ops:
  0.0 11.8 %all-to-all-start.1 = ((bf16[8,64,2048]{2,0,1:T(8,128)(2,1)}), bf16[8,64,2048]{2,0,1:T(8,128)(2,1)}, u32[]{:S(2)}, u32[]{:S(2)}) async-start(bf16[8,64,2048]{2,0,1:T(8,128)(2,1)} %bitcast.28), calls=%async_computation.1 | async-start | bytes 4194304 | tf_op jit(solution)/shard_map/all_to_all | solution.py:157
  11.8 1.3 %dynamic_slice.11 = f32[2048]{0:T(1024)} dynamic-slice(f32[131072]{0:T(1024)} %param.10, s32[]{:T(128)S(6)} %select_n.9), dynamic_slice_sizes={2048} | dynamic-slice | bytes 16388 | tf_op jit(solution)/shard_map/dynamic_slice | solution.py:176
  13.1 1.3 %dynamic_slice.12 = s32[2048]{0:T(1024)} dynamic-slice(s32[131072]{0:T(1024)} %param.11, s32[]{:T(128)S(6)} %select_n.9), dynamic_slice_sizes={2048} | dynamic-slice | bytes 16388 | tf_op jit(solution)/shard_map/dynamic_slice | solution.py:177
  14.4 2.2 %pad_maximum_fusion = bf16[8,64,3072]{2,0,1:T(8,128)(2,1)S(1)} fusion(bf16[8,64,1024]{2,0,1:T(8,128)(2,1)} %bitcast.29, bf16[8,64,2048]{2,0,1:T(8,128)(2,1)} %bitcast.27), kind=kLoop, calls=%fused_computation | loop fusion | flops 6291456 | bytes 6291456 | tf_op jit(solution)/shard_map/concatenate | solution.py:182
  16.6 0.0 copy-start.1
  16.6 1.9 %rev.8 = bf16[8,64,3072]{2,0,1:T(8,128)(2,1)} reverse(bf16[8,64,3072]{2,0,1:T(8,128)(2,1)S(1)} %pad_maximum_fusion), dimensions={1} | reverse | bytes 6291456 | tf_op jit(solution)/shard_map/jit(_flip)/rev | solution.py:185
  18.5 0.0 copy-done.1
  18.5 0.6 pad_add_fusion.scalars
  19.1 1.8 %factor_kernel.1.factor = f32[2,2048]{1,0:T(2,128)} custom-call(s32[3]{0:T(128)} %pad_add_fusion.scalars, s32[2,2048]{1,0:T(2,128)} %bitcast.32, f32[1,2048]{1,0:T(1,128)} %bitcast.30, s32[1,2048]{1,0:T(1,128)} %bitcast.31), custom_call_target="tpu_custom_call" | custom-call | flops 536870912 | bytes 4194304 | tf_op jit(solution)/shard_map/factor_kernel/pallas_call | solution.py:140
  20.9 20.7 %all-to-all-done.1 = bf16[8,64,2048]{2,0,1:T(8,128)(2,1)} async-done(((bf16[8,64,2048]{2,0,1:T(8,128)(2,1)}), bf16[8,64,2048]{2,0,1:T(8,128)(2,1)}, u32[]{:S(2)}, u32[]{:S(2)}) %all-to-all-start.1) | async-done | bytes 2097184 | tf_op jit(solution)/shard_map/all_to_all | solution.py:157
  41.6 9.8 %all-to-all-start = ((bf16[8,64,3072]{2,0,1:T(8,128)(2,1)}), bf16[8,64,3072]{2,0,1:T(8,128)(2,1)S(1)}, u32[]{:S(2)}, u32[]{:S(2)}) async-start(bf16[8,64,3072]{2,0,1:T(8,128)(2,1)} %rev.8), calls=%async_computation | async-start | bytes 6291456 | tf_op jit(solution)/shard_map/all_to_all | solution.py:157
  51.4 0.0 copy-start
  51.4 26.7 %gain_kernel.1.gain = bf16[2048,1024]{1,0:T(8,128)(2,1)} custom-call(bf16[512,2048]{1,0:T(8,128)(2,1)} %bitcast.13.pred, f32[2,2048]{1,0:T(2,128)} %factor_kernel.1.factor), custom_call_target="tpu_custom_call" | custom-call | flops 21474836480 | bytes 4194304 | tf_op jit(solution)/shard_map/gain_kernel/pallas_call | solution.py:140
  78.1 7.0 %all-to-all-done = bf16[8,64,3072]{2,0,1:T(8,128)(2,1)S(1)} async-done(((bf16[8,64,3072]{2,0,1:T(8,128)(2,1)}), bf16[8,64,3072]{2,0,1:T(8,128)(2,1)S(1)}, u32[]{:S(2)}, u32[]{:S(2)}) %all-to-all-start) | async-done | bytes 3145760 | tf_op jit(solution)/shard_map/all_to_all | solution.py:157
  85.1 0.0 copy-done
  85.1 5.4 %update_kernel.1 = bf16[512,1024]{1,0:T(8,128)(2,1)S(1)} custom-call(bf16[512,3072]{1,0:T(8,128)(2,1)S(1)} %bitcast.24, f32[2,2048]{1,0:T(2,128)S(1)} %copy-done, bf16[512,2048]{1,0:T(8,128)(2,1)} %bitcast.13.pred, bf16[2048,1024]{1,0:T(8,128)(2,1)} %gain_kernel.1.gain), custom_call_target="tpu_custom_call" | custom-call | flops 2684354560 | bytes 4194304 | tf_op jit(solution)/shard_map/update_kernel/pallas_call | solution.py:140
  90.5 23.9 %all_to_all.46 = bf16[64,8,1024]{2,1,0:T(8,128)(2,1)S(1)} all-to-all(bf16[64,8,1024]{2,1,0:T(8,128)(2,1)S(1)} %bitcast.25), channel_id=1, replica_groups={{64,66,68,70,72,74,76,78,80,82,84,86,88,90,92,94,96,98,100,102,104,106,..., dimensions={0} | all-to-all | bytes 2097152 | tf_op jit(solution)/shard_map/all_to_all | solution.py:209
  114.4 1.0 rev.9
  (1 shorter events, 0.0 us)
Async XLA Ops:
  0.0 41.6 %all-to-all-start.1 = ((bf16[8,64,2048]{2,0,1:T(8,128)(2,1)}), bf16[8,64,2048]{2,0,1:T(8,128)(2,1)}, u32[]{:S(2)}, u32[]{:S(2)}) async-start(bf16[8,64,2048]{2,0,1:T(8,128)(2,1)} %bitcast.28), calls=%async_computation.1 | async-start | bytes 4194304 | tf_op jit(solution)/shard_map/all_to_all | solution.py:157
  16.6 1.9 %copy-start.1 = (s32[2,2]{1,0:T(2,128)S(1)}, s32[2,2]{1,0:T(2,128)}, u32[]{:S(2)}) copy-start(s32[2,2]{1,0:T(2,128)} %param.12) | copy-start | bytes 52
  41.6 43.5 %all-to-all-start = ((bf16[8,64,3072]{2,0,1:T(8,128)(2,1)}), bf16[8,64,3072]{2,0,1:T(8,128)(2,1)S(1)}, u32[]{:S(2)}, u32[]{:S(2)}) async-start(bf16[8,64,3072]{2,0,1:T(8,128)(2,1)} %rev.8), calls=%async_computation | async-start | bytes 6291456 | tf_op jit(solution)/shard_map/all_to_all | solution.py:157
  51.4 33.7 %copy-start = (f32[2,2048]{1,0:T(2,128)S(1)}, f32[2,2048]{1,0:T(2,128)}, u32[]{:S(2)}) copy-start(f32[2,2048]{1,0:T(2,128)} %factor_kernel.1.factor) | copy-start | bytes 49156
